TPU v7x, 32 devices: a whole 2x2x4 slice. The times are simulated.
32 devices in a mesh: dp: 8 (over z, core), tp: 4 (over y, x).
Axes of the slice: x: 2, y: 2, z: 4, core: 2. Of those that a mesh axis runs over, the one named last changes fastest.
Arguments:
- master: float32 [4096, 10240], P(('dp', 'tp')), may hold values from -0.09375 to 0.09375
- grad: float32 [4096, 10240], P(('dp', 'tp')), may hold values from -0.006 to 0.006
- exp_avg: float32 [4096, 10240], P(('dp', 'tp')), may hold values from -0.006 to 0.006
- exp_avg_sq: float32 [4096, 10240], P(('dp', 'tp')), may hold values from 1e-08 to 1e-05
Outputs:
- new_master: float32 [4096, 10240], P(('dp', 'tp'))
- new_avg: float32 [4096, 10240], P(('dp', 'tp'))
- new_avg_sq: float32 [4096, 10240], P(('dp', 'tp'))
- engine_qkv: bfloat16 [4096, 10240], P(None, 'tp')
All inputs are finite; a program needn't handle non-finite values.
Results may differ from a plain program's by a relative error of at most 0.001.
Values may be sent and summed in bfloat16 or wider, within the bound.
A program may use at most 128 MiB of HBM per device.

v0:
```python
import functools

import jax
import jax.numpy as jnp
from jax import lax
from jax.experimental import pallas as pl
from jax.experimental.pallas import tpu as pltpu
from jax.sharding import PartitionSpec as P

QH = 64
KVH = 8
HS = 128
CORES = 2
MESH = pl.DeviceIdType.MESH


def step_math(master, grad, exp_avg, exp_avg_sq):
    corr_one = 1.0 - 0.9**10
    corr_two = 1.0 - 0.999**10
    new_avg = 0.9 * exp_avg + 0.1 * grad
    new_avg_sq = 0.999 * exp_avg_sq + 0.001 * grad * grad
    update = new_avg / corr_one / (jnp.sqrt(new_avg_sq / corr_two) + 1e-08)
    new_master = master - 0.001 * (update + 0.1 * master)
    return new_master, new_avg, new_avg_sq


def pieces_of(tp_count):
    q, kv = QH // tp_count * HS, KVH // tp_count * HS
    return [
        [(t * q, q, 0), (QH * HS + t * kv, kv, q), ((QH + KVH) * HS + t * kv, kv, q + kv)]
        for t in range(tp_count)
    ]


def step_kernel(tp_count, m_ref, g_ref, a_ref, s_ref, first_ref, nm_ref, na_ref, ns_ref, out_ref):
    for t, pieces in enumerate(pieces_of(tp_count)):
        for start, width, into in pieces:
            cols = pl.ds(start, width)
            new_master, new_avg, new_avg_sq = step_math(
                m_ref[:, cols], g_ref[:, cols], a_ref[:, cols], s_ref[:, cols]
            )
            nm_ref[:, cols] = new_master
            na_ref[:, cols] = new_avg
            ns_ref[:, cols] = new_avg_sq
            out_ref[t, :, pl.ds(into, width)] = new_master.astype(jnp.bfloat16)


def local_step(tp_count, master, grad, exp_avg, exp_avg_sq, first):
    rows, cols = master.shape
    tile = 16
    flat = pl.BlockSpec((tile, cols), lambda i: (i, 0))
    f32 = jax.ShapeDtypeStruct((rows, cols), jnp.float32)
    return pl.pallas_call(
        functools.partial(step_kernel, tp_count),
        grid=(rows // tile,),
        in_specs=[flat] * 4 + [pl.BlockSpec(memory_space=pltpu.HBM)],
        out_specs=[flat] * 3 + [pl.BlockSpec((tp_count, tile, cols // tp_count), lambda i: (0, i, 0))],
        out_shape=[f32] * 3 + [jax.ShapeDtypeStruct((tp_count, rows, cols // tp_count), jnp.bfloat16)],
        compiler_params=pltpu.CompilerParams(vmem_limit_bytes=56 * 2**20),
        cost_estimate=pl.CostEstimate(flops=20 * rows * cols, bytes_accessed=30 * rows * cols, transcendentals=rows * cols),
    )(master, grad, exp_avg, exp_avg_sq, first)


def own_kernel(tp_count, chunks, *refs):
    sources, (out_ref, token_ref), held, sems = refs[:4], refs[4:6], refs[6:10], refs[10]
    t = lax.axis_index("tp")
    q, kv = QH // tp_count * HS, KVH // tp_count * HS
    pieces = [(t * q, q, 0), (QH * HS + t * kv, kv, q), ((QH + KVH) * HS + t * kv, kv, q + kv)]
    rows = out_ref.shape[0] // chunks
    copies = []
    for c in range(chunks):
        part = pl.ds(c * rows, rows)
        for n in range(4):
            for k, (start, width, into) in enumerate(pieces):
                copies.append(
                    pltpu.make_async_copy(
                        sources[n].at[part, pl.ds(pl.multiple_of(start, HS), width)],
                        held[n].at[part, pl.ds(into, width)],
                        sems.at[(c * 4 + n) * 3 + k],
                    )
                )
    for cp in copies:
        cp.start()
    for c in range(chunks):
        for cp in copies[c * 12 : (c + 1) * 12]:
            cp.wait()
        part = pl.ds(c * rows, rows)
        out_ref[part, :] = step_math(*[ref[part, :] for ref in held])[0].astype(jnp.bfloat16)
    token_ref[...] = jnp.zeros_like(token_ref)


def own_slice(tp_count, *arrays):
    rows, cols = arrays[0].shape
    width = cols // tp_count
    chunks = max(rows // 32, 1)
    vmem = pl.BlockSpec(memory_space=pltpu.VMEM)
    return pl.pallas_call(
        functools.partial(own_kernel, tp_count, chunks),
        in_specs=[pl.BlockSpec(memory_space=pltpu.HBM)] * 4,
        out_specs=[vmem, vmem],
        out_shape=[jax.ShapeDtypeStruct((rows, width), jnp.bfloat16), jax.ShapeDtypeStruct((8, 128), jnp.float32)],
        scratch_shapes=[pltpu.VMEM((rows, width), jnp.float32)] * 4 + [pltpu.SemaphoreType.DMA((chunks * 12,))],
        compiler_params=pltpu.CompilerParams(vmem_limit_bytes=60 * 2**20),
        cost_estimate=pl.CostEstimate(flops=20 * rows * width, bytes_accessed=18 * rows * width, transcendentals=rows * width),
    )(*arrays)


def mix(t, j, count):
    out, bit = 0, 1
    while bit < count:
        out = out + ((t // bit) % 2 + (j // bit) % 2) % 2 * bit
        bit *= 2
    return out


def spread_kernel(dp_count, tp_count, parts, own_ref, below_ref, above_ref, out_ref, own_sem, flat_send, up_send, down_send, side_send, in_recv, side_recv):
    planes = dp_count // CORES
    dp, t = lax.axis_index("dp"), lax.axis_index("tp")
    z, core = dp // CORES, dp % CORES
    rows = own_ref.shape[1]
    part_rows = rows // parts
    has_up, has_down = z < planes - 1, z > 0
    units = tp_count * parts

    up = {"dp": dp + CORES}
    down = {"dp": dp - CORES}
    side = {"dp": z * CORES + 1 - core}

    barrier = pltpu.get_barrier_semaphore()
    for j in range(1, tp_count):
        pl.semaphore_signal(barrier, inc=1, device_id={"tp": mix(t, j, tp_count)}, device_id_type=MESH)
    pl.semaphore_signal(barrier, inc=1, device_id=side, device_id_type=MESH)

    @pl.when(has_up)
    def _():
        pl.semaphore_signal(barrier, inc=1, device_id=up, device_id_type=MESH)

    @pl.when(has_down)
    def _():
        pl.semaphore_signal(barrier, inc=1, device_id=down, device_id_type=MESH)

    pl.semaphore_wait(barrier, tp_count + has_up.astype(jnp.int32) + has_down.astype(jnp.int32))

    def place(plane, which_core, unit):
        source = mix(t, unit // parts, tp_count)
        block = (plane * CORES + which_core) * tp_count + source
        start = block * rows + unit % parts * part_rows
        return out_ref.at[pl.ds(pl.multiple_of(start, part_rows), part_rows), :]

    def copy(src, dst, send, recv, target):
        return pltpu.make_async_remote_copy(
            src_ref=src, dst_ref=dst, send_sem=send, recv_sem=recv, device_id=target, device_id_type=MESH
        )

    def going_up(src, plane, unit):
        return copy(src, place(plane, core, unit), up_send.at[plane, unit], in_recv.at[plane, unit], up)

    def going_down(src, plane, unit):
        return copy(src, place(plane, core, unit), down_send.at[plane, unit], in_recv.at[plane, unit], down)

    def going_side(src, plane, unit):
        return copy(src, place(plane, core, unit), side_send.at[plane, unit], side_recv.at[plane, unit], side)

    def arrived(plane, unit):
        here = place(plane, core, unit)
        copy(here, here, side_send.at[plane, unit], in_recv.at[plane, unit], side).wait_recv()

    def own_part(which, h):
        return own_ref.at[which, pl.ds(h * part_rows, part_rows), :]

    def flat_copy(j, h):
        target = mix(t, j, tp_count)
        start = ((z * CORES + core) * tp_count + t) * rows + h * part_rows
        dst = out_ref.at[pl.ds(pl.multiple_of(start, part_rows), part_rows), :]
        unit = j * parts + h
        return copy(own_part(target, h), dst, flat_send.at[unit], in_recv.at[z, unit], {"tp": target})

    def onward(src, unit):
        @pl.when(has_up)
        def _():
            going_up(src, z, unit).start()

        @pl.when(has_down)
        def _():
            going_down(src, z, unit).start()

    def given(ref, h):
        return ref.at[pl.ds(h * part_rows, part_rows), :]

    def keep(which, src, plane, h):
        return pltpu.make_async_copy(src, place(plane, core, h), own_sem.at[which, h])

    for h in range(parts):

        @pl.when(has_up & has_down)
        def _():
            going_up(given(below_ref, h), z - 1, h).start()
            going_down(given(above_ref, h), z + 1, h).start()

        for j in range(1, tp_count):
            flat_copy(j, h).start()
    for h in range(parts):
        keep(0, own_part(t, h), z, h).start()
        going_side(own_part(t, h), z, h).start()

        @pl.when(has_down)
        def _():
            keep(1, given(below_ref, h), z - 1, h).start()
            going_side(given(below_ref, h), z - 1, h).start()

        @pl.when(has_up)
        def _():
            keep(2, given(above_ref, h), z + 1, h).start()
            going_side(given(above_ref, h), z + 1, h).start()

    @pl.loop(parts, units)
    def _(unit):
        arrived(z, unit)
        onward(place(z, core, unit), unit)
        going_side(place(z, core, unit), z, unit).start()

    @pl.loop(parts, (planes - 1) * units)
    def _(m):
        distance, unit = m // units + 1, m % units
        below, above = z - distance, z + distance

        @pl.when(below >= 0)
        def _():
            arrived(below, unit)

            @pl.when(has_up)
            def _():
                going_up(place(below, core, unit), below, unit).start()

            going_side(place(below, core, unit), below, unit).start()

        @pl.when(above < planes)
        def _():
            arrived(above, unit)

            @pl.when(has_down)
            def _():
                going_down(place(above, core, unit), above, unit).start()

            going_side(place(above, core, unit), above, unit).start()

    for h in range(parts):
        keep(0, own_part(t, h), z, h).wait()

        @pl.when(has_down)
        def _():
            keep(1, given(below_ref, h), z - 1, h).wait()

        @pl.when(has_up)
        def _():
            keep(2, given(above_ref, h), z + 1, h).wait()

    for j in range(1, tp_count):
        for h in range(parts):
            flat_copy(j, h).wait_send()

    @pl.loop(0, planes * units)
    def _(m):
        plane, unit = m // units, m % units
        here = place(plane, core, unit)
        there = place(plane, 1 - core, unit)

        early = (plane == z) & (unit < parts)

        @pl.when((plane <= z) & has_up & jnp.logical_not(early))
        def _():
            going_up(here, plane, unit).wait_send()

        @pl.when((plane >= z) & has_down & jnp.logical_not(early))
        def _():
            going_down(here, plane, unit).wait_send()

        going_side(here, plane, unit).wait_send()
        copy(there, there, side_send.at[plane, unit], side_recv.at[plane, unit], side).wait_recv()


def spread(dp_count, tp_count, own, below, above):
    rows, width = own.shape[1:]
    parts = 2 if rows % 64 == 0 else 1
    planes, units = dp_count // CORES, tp_count * parts
    grid = pltpu.SemaphoreType.DMA((planes, units))
    return pl.pallas_call(
        functools.partial(spread_kernel, dp_count, tp_count, parts),
        in_specs=[pl.BlockSpec(memory_space=pltpu.HBM)] * 3,
        out_specs=pl.BlockSpec(memory_space=pl.ANY),
        out_shape=jax.ShapeDtypeStruct((dp_count * tp_count * rows, width), jnp.bfloat16),
        scratch_shapes=[pltpu.SemaphoreType.DMA((3, parts)), pltpu.SemaphoreType.DMA((units,))] + [grid] * 5,
        compiler_params=pltpu.CompilerParams(collective_id=0, has_side_effects=True, vmem_limit_bytes=4 * 2**20),
        cost_estimate=pl.CostEstimate(flops=0, bytes_accessed=2 * dp_count * tp_count * rows * width, transcendentals=0),
    )(own, below, above)


def body(dp_count, tp_count, master, grad, exp_avg, exp_avg_sq):
    first, token = own_slice(tp_count, master, grad, exp_avg, exp_avg_sq)
    rise = [(i, i + CORES) for i in range(dp_count - CORES)]
    below = lax.ppermute(first, "dp", rise)
    above = lax.ppermute(first, "dp", [(b, a) for a, b in rise])
    new_master, new_avg, new_avg_sq, own = local_step(tp_count, master, grad, exp_avg, exp_avg_sq, token)
    return new_master, new_avg, new_avg_sq, spread(dp_count, tp_count, own, below, above)


def solution(mesh):
    flat = P(("dp", "tp"), None)
    return jax.shard_map(
        functools.partial(body, mesh.shape["dp"], mesh.shape["tp"]),
        mesh=mesh,
        in_specs=(flat,) * 4,
        out_specs=(flat, flat, flat, P(None, "tp")),
        check_vma=False,
    )
```

profile of v0, /device:TPU:0, one launch (start us, length us, event | category | flops | bytes accessed | tf_op | source)
XLA Modules:
  0.0 198.7 jit_solution(3211568845458976902)
XLA Ops:
  0.6 4.0 %shard_map.75 = (bf16[128,2560]{1,0:T(8,128)(2,1)}, f32[8,128]{1,0:T(8,128)}) custom-call(f32[128,10240]{1,0:T(8,128)} %m_ref.1, f32[128,10240]{1,0:T(8,128)} %g_ref.1, f32[128,10240]{1,0:T(8,128)} %a_ref.1, f32[128,10240]{1,0:T(8,128)} %s_ref.1), custom_call_target="tpu_custom_call" | custom-call | flops 6553600 | bytes 5898240 | tf_op jit(solution)/shard_map/pallas_call | solution.py:97
  4.7 1.3 collective-permute-start.1
  6.0 5.6 %collective-permute-start = (bf16[128,2560]{1,0:T(8,128)(2,1)}, bf16[128,2560]{1,0:T(8,128)(2,1)S(1)}, u32[]{:S(2)}, u32[]{:S(2)}) collective-permute-start(bf16[128,2560]{1,0:T(8,128)(2,1)} %get-tuple-element.15), channel_id=1, source_target_pairs={{0,8},{4,12},{8,16},{12,20},{16,24},{20,28},{1,9},{5,13},{9,17},{1... | collective-permute-start | bytes 1966088 | tf_op jit(solution)/shard_map/ppermute | solution.py:301
  11.6 16.2 %shard_map.76 = (f32[128,10240]{1,0:T(8,128)}, f32[128,10240]{1,0:T(8,128)}, f32[128,10240]{1,0:T(8,128)}, bf16[4,128,2560]{2,1,0:T(8,128)(2,1)}) custom-call(f32[128,10240]{1,0:T(8,128)} %m_ref.1, f32[128,10240]{1,0:T(8,128)} %g_ref.1, f32[128,10240]{1,0:T(8,128)} %a_ref.1, f32[128,10240]{1,0:T(8,128)} %s_ref.1, f32[8,128]{1,0:T(8,128)} %get-tuple-element.10.first_ref), custom_call_target="tpu_custom_call" | custom-call | flops 26214400 | bytes 39321600 | tf_op jit(solution)/shard_map/pallas_call | solution.py:53
  27.8 0.0 collective-permute-done.1.above_ref
  27.8 0.0 collective-permute-done.below_ref
  27.8 0.0 copy-start
  27.8 1.7 copy-done
  29.5 161.6 %shard_map.77 = bf16[4096,2560]{1,0:T(8,128)(2,1)S(1)} custom-call(bf16[4,128,2560]{2,1,0:T(8,128)(2,1)S(1)} %copy-done, bf16[128,2560]{1,0:T(8,128)(2,1)S(1)} %collective-permute-done.below_ref, bf16[128,2560]{1,0:T(8,128)(2,1)S(1)} %collective-permute-done.1.above_ref), custom_call_target="tpu_custom_call" | custom-call | bytes 20971520 | tf_op jit(solution)/shard_map/pallas_call | solution.py:287
  191.1 7.5 %copy.9 = bf16[4096,2560]{1,0:T(8,128)(2,1)} copy(bf16[4096,2560]{1,0:T(8,128)(2,1)S(1)} %shard_map.77) | data formatting | bytes 41943040
Async XLA Ops:
  4.7 23.1 %collective-permute-start.1 = (bf16[128,2560]{1,0:T(8,128)(2,1)}, bf16[128,2560]{1,0:T(8,128)(2,1)S(1)}, u32[]{:S(2)}, u32[]{:S(2)}) collective-permute-start(bf16[128,2560]{1,0:T(8,128)(2,1)} %get-tuple-element.15), channel_id=1, source_target_pairs={{8,0},{12,4},{16,8},{20,12},{24,16},{28,20},{9,1},{13,5},{17,9},{2... | collective-permute-start | bytes 1966088 | tf_op jit(solution)/shard_map/ppermute | solution.py:302
  6.0 21.8 %collective-permute-start = (bf16[128,2560]{1,0:T(8,128)(2,1)}, bf16[128,2560]{1,0:T(8,128)(2,1)S(1)}, u32[]{:S(2)}, u32[]{:S(2)}) collective-permute-start(bf16[128,2560]{1,0:T(8,128)(2,1)} %get-tuple-element.15), channel_id=1, source_target_pairs={{0,8},{4,12},{8,16},{12,20},{16,24},{20,28},{1,9},{5,13},{9,17},{1... | collective-permute-start | bytes 1966088 | tf_op jit(solution)/shard_map/ppermute | solution.py:301
  27.8 1.7 copy-start
where the time goes:
time: 199 us
  Pallas kernels  182 us (91%)
  local copies, waits for them, and re-layouts  9.28 us (5%)
  starting transfers between devices  6.92 us (3%)
    pallas_call x1, Pallas kernels, spread(): pl.pallas_call(functools.partial(spread_kernel, dp_count, tp_count, parts...  162 us
    pallas_call x1, Pallas kernels, local_step(): pl.pallas_call(functools.partial(step_kernel, tp_count), grid=(rows // ti...  16.2 us
    unnamed x3, local copies, waits for them, and re-layouts  9.28 us
    ppermute x1, starting transfers between devices, body(): below = lax.ppermute(first, 'dp', rise)  5.62 us
    pallas_call x1, Pallas kernels, own_slice(): pl.pallas_call(functools.partial(own_kernel, tp_count, chunks), in_specs=...  4.03 us
  transfers between devices with their start and end apart: 2, of which 0 were waited for; matrix products, arithmetic and copies ran while one was open for 0% of the time, Pallas kernels for 8%

commit v1 on v0

v1 whole, which is shorter than its diff:
```python
import functools

import jax
import jax.numpy as jnp
from jax import lax
from jax.experimental import pallas as pl
from jax.experimental.pallas import tpu as pltpu
from jax.sharding import PartitionSpec as P

QH = 64
KVH = 8
HS = 128
CORES = 2
STEP = 16
MESH = pl.DeviceIdType.MESH


def step_math(master, grad, exp_avg, exp_avg_sq):
    corr_one = 1.0 - 0.9**10
    corr_two = 1.0 - 0.999**10
    new_avg = 0.9 * exp_avg + 0.1 * grad
    new_avg_sq = 0.999 * exp_avg_sq + 0.001 * grad * grad
    update = new_avg / corr_one / (jnp.sqrt(new_avg_sq / corr_two) + 1e-08)
    new_master = master - 0.001 * (update + 0.1 * master)
    return new_master, new_avg, new_avg_sq


def pieces_of(tp_count, t):
    q, kv = QH // tp_count * HS, KVH // tp_count * HS
    return [(t * q, q, 0), (QH * HS + t * kv, kv, q), ((QH + KVH) * HS + t * kv, kv, q + kv)]


def mix(t, j, count):
    out, bit = 0, 1
    while bit < count:
        out = out + ((t // bit) % 2 + (j // bit) % 2) % 2 * bit
        bit *= 2
    return out


def parts_of(rows):
    return 2 if rows % 64 == 0 else 1


def jobs_of(tp_count, rows):
    part_rows = rows // parts_of(rows)
    jobs, start = [], 0
    first = [STEP, STEP]
    while sum(first) < part_rows:
        first.append(min(sum(first), part_rows - sum(first)))
    for size in first + [part_rows] * (rows // part_rows - 1):
        jobs.append((0, start, size))
        start += size
    for j in range(1, tp_count):
        for h in range(rows // part_rows):
            jobs.append((j, h * part_rows, part_rows))
    return jobs


def spread_kernel(dp_count, tp_count, parts, *refs):
    sources, out_ref, held, mine, load_sem = refs[:4], refs[4], refs[5], refs[6], refs[7]
    own_sem, flat_send, up_send, down_send, side_send, in_recv, side_recv = refs[8:]
    planes = dp_count // CORES
    dp, t = lax.axis_index("dp"), lax.axis_index("tp")
    z, core = dp // CORES, dp % CORES
    rows = mine.shape[1]
    part_rows = rows // parts
    has_up, has_down = z < planes - 1, z > 0
    units = tp_count * parts

    up = {"dp": dp + CORES}
    down = {"dp": dp - CORES}
    side = {"dp": z * CORES + 1 - core}

    barrier = pltpu.get_barrier_semaphore()
    for j in range(1, tp_count):
        pl.semaphore_signal(barrier, inc=1, device_id={"tp": mix(t, j, tp_count)}, device_id_type=MESH)
    pl.semaphore_signal(barrier, inc=1, device_id=side, device_id_type=MESH)

    @pl.when(has_up)
    def _():
        pl.semaphore_signal(barrier, inc=1, device_id=up, device_id_type=MESH)

    @pl.when(has_down)
    def _():
        pl.semaphore_signal(barrier, inc=1, device_id=down, device_id_type=MESH)

    jobs = jobs_of(tp_count, rows)

    def loads(i):
        j, first, size = jobs[i]
        part = pl.ds(first, size)
        return [
            pltpu.make_async_copy(
                sources[n].at[part, pl.ds(pl.multiple_of(start, HS), width)],
                held.at[j, n, part, pl.ds(into, width)],
                load_sem.at[(i * 4 + n) * 3 + k],
            )
            for n in range(4)
            for k, (start, width, into) in enumerate(pieces_of(tp_count, mix(t, j, tp_count)))
        ]

    def compute(i):
        j, first, size = jobs[i]

        def rows_at(start):
            part = pl.ds(start, STEP)
            new_master = step_math(*[held[j, n, part, :] for n in range(4)])[0]
            mine[j, part, :] = new_master.astype(jnp.bfloat16)

        if size == STEP:
            rows_at(first)
        else:

            @pl.loop(0, size // STEP)
            def _(k):
                rows_at(pl.multiple_of(first + k * STEP, STEP))

    def place(plane, which_core, unit):
        source = mix(t, unit // parts, tp_count)
        block = (plane * CORES + which_core) * tp_count + source
        start = block * rows + unit % parts * part_rows
        return out_ref.at[pl.ds(pl.multiple_of(start, part_rows), part_rows), :]

    def copy(src, dst, send, recv, target):
        return pltpu.make_async_remote_copy(
            src_ref=src, dst_ref=dst, send_sem=send, recv_sem=recv, device_id=target, device_id_type=MESH
        )

    def going_up(src, dst, plane, unit):
        return copy(src, dst, up_send.at[plane, unit], in_recv.at[plane, unit], up)

    def going_down(src, dst, plane, unit):
        return copy(src, dst, down_send.at[plane, unit], in_recv.at[plane, unit], down)

    def going_side(src, dst, plane, unit):
        return copy(src, dst, side_send.at[plane, unit], side_recv.at[plane, unit], side)

    def arrived(plane, unit):
        here = place(plane, core, unit)
        copy(here, here, side_send.at[plane, unit], in_recv.at[plane, unit], side).wait_recv()

    def home(first, size):
        start = ((z * CORES + core) * tp_count + t) * rows + first
        return out_ref.at[pl.ds(pl.multiple_of(start, STEP), size), :]

    def flat_copy(j, h):
        part = pl.ds(h * part_rows, part_rows)
        unit = j * parts + h
        target = {"tp": mix(t, j, tp_count)}
        return copy(mine.at[j, part, :], home(h * part_rows, part_rows), flat_send.at[unit], in_recv.at[z, unit], target)

    def keep(h):
        return pltpu.make_async_copy(mine.at[0, pl.ds(h * part_rows, part_rows), :], place(z, core, h), own_sem.at[h])

    def send(i):
        j, first, size = jobs[i]
        h = first // part_rows
        if j > 0:
            flat_copy(j, h).start()
            return
        src, dst = mine.at[0, pl.ds(first, size), :], home(first, size)

        @pl.when(has_up)
        def _():
            going_up(src, dst, z, h).start()

        @pl.when(has_down)
        def _():
            going_down(src, dst, z, h).start()

        going_side(src, dst, z, h).start()
        if (first + size) % part_rows == 0:
            keep(h).start()

    ahead = 2
    for i in range(ahead):
        for cp in loads(i):
            cp.start()
    for i in range(len(jobs)):
        for cp in loads(i):
            cp.wait()
        if i + ahead < len(jobs):
            for cp in loads(i + ahead):
                cp.start()
        compute(i)
        if i == 0:
            pl.semaphore_wait(barrier, tp_count + has_up.astype(jnp.int32) + has_down.astype(jnp.int32))
        else:
            send(i - 1)
    send(len(jobs) - 1)

    @pl.loop(parts, units)
    def _(unit):
        arrived(z, unit)
        here = place(z, core, unit)

        @pl.when(has_up)
        def _():
            going_up(here, here, z, unit).start()

        @pl.when(has_down)
        def _():
            going_down(here, here, z, unit).start()

        going_side(here, here, z, unit).start()

    @pl.loop(0, (planes - 1) * units)
    def _(m):
        distance, unit = m // units + 1, m % units
        below, above = z - distance, z + distance

        @pl.when(below >= 0)
        def _():
            arrived(below, unit)
            here = place(below, core, unit)

            @pl.when(has_up)
            def _():
                going_up(here, here, below, unit).start()

            going_side(here, here, below, unit).start()

        @pl.when(above < planes)
        def _():
            arrived(above, unit)
            here = place(above, core, unit)

            @pl.when(has_down)
            def _():
                going_down(here, here, above, unit).start()

            going_side(here, here, above, unit).start()

    for h in range(parts):
        keep(h).wait()
    for j in range(1, tp_count):
        for h in range(parts):
            flat_copy(j, h).wait_send()

    @pl.loop(0, planes * units)
    def _(m):
        plane, unit = m // units, m % units
        here = place(plane, core, unit)
        there = place(plane, 1 - core, unit)

        @pl.when((plane <= z) & has_up)
        def _():
            going_up(here, here, plane, unit).wait_send()

        @pl.when((plane >= z) & has_down)
        def _():
            going_down(here, here, plane, unit).wait_send()

        going_side(here, here, plane, unit).wait_send()
        copy(there, there, side_send.at[plane, unit], side_recv.at[plane, unit], side).wait_recv()


def spread(dp_count, tp_count, *arrays):
    rows, cols = arrays[0].shape
    width = cols // tp_count
    parts = parts_of(rows)
    planes, units = dp_count // CORES, tp_count * parts
    grid = pltpu.SemaphoreType.DMA((planes, units))
    jobs = len(jobs_of(tp_count, rows))
    return pl.pallas_call(
        functools.partial(spread_kernel, dp_count, tp_count, parts),
        in_specs=[pl.BlockSpec(memory_space=pltpu.HBM)] * 4,
        out_specs=pl.BlockSpec(memory_space=pl.ANY),
        out_shape=pltpu.VMEM((dp_count * tp_count * rows, width), jnp.bfloat16),
        scratch_shapes=[
            pltpu.VMEM((tp_count, 4, rows, width), jnp.float32),
            pltpu.VMEM((tp_count, rows, width), jnp.bfloat16),
            pltpu.SemaphoreType.DMA((jobs * 12,)),
            pltpu.SemaphoreType.DMA((parts,)),
            pltpu.SemaphoreType.DMA((units,)),
        ]
        + [grid] * 5,
        compiler_params=pltpu.CompilerParams(collective_id=0, has_side_effects=True, vmem_limit_bytes=28 * 2**20),
        cost_estimate=pl.CostEstimate(flops=20 * rows * cols, bytes_accessed=16 * rows * cols, transcendentals=rows * cols),
    )(*[pltpu.with_memory_space_constraint(x, pltpu.HBM) for x in arrays])


def step_kernel(m_ref, g_ref, a_ref, s_ref, all_ref, nm_ref, na_ref, ns_ref, engine_ref, sems):
    count = sems.shape[0]
    rows = engine_ref.shape[0] // count

    def whole(n):
        part = pl.ds(n * rows, rows)
        return pltpu.make_async_copy(all_ref.at[part, :], engine_ref.at[part, :], sems.at[n])

    @pl.when(pl.program_id(0) == 0)
    def _():
        for n in range(count):
            whole(n).start()

    new_master, new_avg, new_avg_sq = step_math(m_ref[...], g_ref[...], a_ref[...], s_ref[...])
    nm_ref[...] = new_master
    na_ref[...] = new_avg
    ns_ref[...] = new_avg_sq

    @pl.when(pl.program_id(0) == pl.num_programs(0) - 1)
    def _():
        for n in range(count):
            whole(n).wait()


def local_step(arrays, gathered):
    rows, cols = arrays[0].shape
    tile = 16
    flat = pl.BlockSpec((tile, cols), lambda i: (i, 0))
    f32 = jax.ShapeDtypeStruct((rows, cols), jnp.float32)
    return pl.pallas_call(
        step_kernel,
        grid=(rows // tile,),
        in_specs=[flat] * 4 + [pl.BlockSpec(memory_space=pl.ANY)],
        out_specs=[flat] * 3 + [pl.BlockSpec(memory_space=pltpu.HBM)],
        out_shape=[f32] * 3 + [jax.ShapeDtypeStruct(gathered.shape, gathered.dtype)],
        scratch_shapes=[pltpu.SemaphoreType.DMA((4,))],
        compiler_params=pltpu.CompilerParams(vmem_limit_bytes=24 * 2**20),
        cost_estimate=pl.CostEstimate(
            flops=20 * rows * cols,
            bytes_accessed=28 * rows * cols + 2 * gathered.size,
            transcendentals=rows * cols,
        ),
    )(*[pltpu.with_memory_space_constraint(x, pltpu.HBM) for x in arrays], pltpu.with_memory_space_constraint(gathered, pltpu.VMEM))


def body(dp_count, tp_count, *arrays):
    gathered = spread(dp_count, tp_count, *arrays)
    return tuple(local_step(arrays, gathered))


def solution(mesh):
    flat = P(("dp", "tp"), None)
    return jax.shard_map(
        functools.partial(body, mesh.shape["dp"], mesh.shape["tp"]),
        mesh=mesh,
        in_specs=(flat,) * 4,
        out_specs=(flat, flat, flat, P(None, "tp")),
        check_vma=False,
    )
```

time: 199 us -> 202 us (1.015)
  Pallas kernels: 182 us -> 201 us
  local copies, waits for them, and re-layouts: 9.28 us -> 0 us
  starting transfers between devices: 6.92 us -> 0 us
    pallas_call x1, Pallas kernels: 162 us -> 179 us  [spread(): pl.pallas_call(functools.partial(spread_kernel, dp_count, tp_count, parts...]
    unnamed x3 -> x0, local copies, waits for them, and re-layouts: 9.28 us -> none
    ppermute x2 -> x0, starting transfers between devices: 6.92 us -> none  [the longest x1 5.62 us: body(): below = lax.ppermute(first, 'dp', rise)]
    pallas_call x2 -> x1, Pallas kernels: 20.2 us -> 22.4 us  [local_step(): pl.pallas_call(step_kernel, grid=(rows // tile,), in_specs=[flat] * 4 + [...]
  transfers between devices with their start and end apart: 2 -> 0, of which waited for: 0 -> 0; matrix products, arithmetic and copies ran while one was open for 0% -> 0% of each run, Pallas kernels for 8% -> 0%
where the time goes in v1:
time: 202 us
  Pallas kernels  201 us (100%)
    pallas_call x1, Pallas kernels, spread(): pl.pallas_call(functools.partial(spread_kernel, dp_count, tp_count, parts...  179 us
    pallas_call x1, Pallas kernels, local_step(): pl.pallas_call(step_kernel, grid=(rows // tile,), in_specs=[flat] * 4 + [...  22.4 us

profile of v1, /device:TPU:0, one launch (start us, length us, event | category | flops | bytes accessed | tf_op | source)
XLA Modules:
  0.0 201.6 jit_solution(15199161870192929190)
XLA Ops:
  0.6 178.5 %shard_map.75.all_ref = bf16[4096,2560]{1,0:T(8,128)(2,1)S(1)} custom-call(f32[128,10240]{1,0:T(8,128)} %m_ref.1, f32[128,10240]{1,0:T(8,128)} %g_ref.1, f32[128,10240]{1,0:T(8,128)} %a_ref.1, f32[128,10240]{1,0:T(8,128)} %s_ref.1), custom_call_target="tpu_custom_call" | custom-call | flops 26214400 | bytes 20971520 | tf_op jit(solution)/shard_map/pallas_call | solution.py:266
  179.2 22.4 %shard_map.76 = (f32[128,10240]{1,0:T(8,128)}, f32[128,10240]{1,0:T(8,128)}, f32[128,10240]{1,0:T(8,128)}, bf16[4096,2560]{1,0:T(8,128)(2,1)}) custom-call(f32[128,10240]{1,0:T(8,128)} %m_ref.1, f32[128,10240]{1,0:T(8,128)} %g_ref.1, f32[128,10240]{1,0:T(8,128)} %a_ref.1, f32[128,10240]{1,0:T(8,128)} %s_ref.1, bf16[4096,2560]{1,0:T(8,128)(2,1)S(1)} %shard_map.75.all_ref), custom_call_target="tpu_custom_call" | custom-call | flops 26214400 | bytes 57671680 | tf_op jit(solution)/shard_map/pallas_call | solution.py:313

commit v2 on v1

--- a/solution.py
+++ b/solution.py
@@ -57,9 +57,9 @@
     return jobs
 
 
-def spread_kernel(dp_count, tp_count, parts, *refs):
-    sources, out_ref, held, mine, load_sem = refs[:4], refs[4], refs[5], refs[6], refs[7]
-    own_sem, flat_send, up_send, down_send, side_send, in_recv, side_recv = refs[8:]
+def spread_kernel(dp_count, tp_count, parts, late, *refs):
+    sources, (out_ref, late_ref), (held, mine, load_sem) = refs[:4], refs[4:6], refs[6:9]
+    own_sem, late_sem, flat_send, up_send, down_send, side_send, in_recv, side_recv = refs[9:]
     planes = dp_count // CORES
     dp, t = lax.axis_index("dp"), lax.axis_index("tp")
     z, core = dp // CORES, dp % CORES
@@ -205,20 +205,31 @@
 
         going_side(here, here, z, unit).start()
 
-    @pl.loop(0, (planes - 1) * units)
+    early = units - late
+
+    def set_aside(here, unit):
+        part = pl.ds(pl.multiple_of((unit - early) * part_rows, part_rows), part_rows)
+        return pltpu.make_async_copy(here, late_ref.at[part, :], late_sem.at[unit - early])
+
+    @pl.loop(0, (planes - 1) * units - late)
     def _(m):
         distance, unit = m // units + 1, m % units
         below, above = z - distance, z + distance
+        keeps = (distance == planes - 2) & (unit >= early)
 
         @pl.when(below >= 0)
         def _():
             arrived(below, unit)
             here = place(below, core, unit)
 
-            @pl.when(has_up)
+            @pl.when(has_up & jnp.logical_not(keeps))
             def _():
                 going_up(here, here, below, unit).start()
 
+            @pl.when(has_up & keeps)
+            def _():
+                set_aside(here, unit).start()
+
             going_side(here, here, below, unit).start()
 
         @pl.when(above < planes)
@@ -226,9 +237,13 @@
             arrived(above, unit)
             here = place(above, core, unit)
 
-            @pl.when(has_down)
+            @pl.when(has_down & jnp.logical_not(keeps))
             def _():
                 going_down(here, here, above, unit).start()
+
+            @pl.when(has_down & keeps)
+            def _():
+                set_aside(here, unit).start()
 
             going_side(here, here, above, unit).start()
 
@@ -244,16 +259,31 @@
         here = place(plane, core, unit)
         there = place(plane, 1 - core, unit)
 
-        @pl.when((plane <= z) & has_up)
+        last = unit >= early
+        held_up = last & (plane == 0) & (z == planes - 2)
+        held_down = last & (plane == planes - 1) & (z == 1)
+        missing = last & ((plane == 0) & (z == planes - 1) | (plane == planes - 1) & (z == 0))
+
+        @pl.when((plane <= z) & has_up & jnp.logical_not(held_up))
         def _():
             going_up(here, here, plane, unit).wait_send()
 
-        @pl.when((plane >= z) & has_down)
+        @pl.when((plane >= z) & has_down & jnp.logical_not(held_down))
         def _():
             going_down(here, here, plane, unit).wait_send()
 
-        going_side(here, here, plane, unit).wait_send()
-        copy(there, there, side_send.at[plane, unit], side_recv.at[plane, unit], side).wait_recv()
+        @pl.when(held_up | held_down)
+        def _():
+            set_aside(here, unit).wait()
+
+        @pl.when(jnp.logical_not(missing))
+        def _():
+            going_side(here, here, plane, unit).wait_send()
+            copy(there, there, side_send.at[plane, unit], side_recv.at[plane, unit], side).wait_recv()
+
+
+def late_of(tp_count, rows):
+    return min(3, tp_count * parts_of(rows) - 1)
 
 
 def spread(dp_count, tp_count, *arrays):
@@ -263,16 +293,21 @@
     planes, units = dp_count // CORES, tp_count * parts
     grid = pltpu.SemaphoreType.DMA((planes, units))
     jobs = len(jobs_of(tp_count, rows))
+    late = late_of(tp_count, rows)
     return pl.pallas_call(
-        functools.partial(spread_kernel, dp_count, tp_count, parts),
+        functools.partial(spread_kernel, dp_count, tp_count, parts, late),
         in_specs=[pl.BlockSpec(memory_space=pltpu.HBM)] * 4,
-        out_specs=pl.BlockSpec(memory_space=pl.ANY),
-        out_shape=pltpu.VMEM((dp_count * tp_count * rows, width), jnp.bfloat16),
+        out_specs=[pl.BlockSpec(memory_space=pl.ANY)] * 2,
+        out_shape=[
+            pltpu.VMEM((dp_count * tp_count * rows, width), jnp.bfloat16),
+            pltpu.VMEM((late * rows // parts, width), jnp.bfloat16),
+        ],
         scratch_shapes=[
             pltpu.VMEM((tp_count, 4, rows, width), jnp.float32),
             pltpu.VMEM((tp_count, rows, width), jnp.bfloat16),
             pltpu.SemaphoreType.DMA((jobs * 12,)),
             pltpu.SemaphoreType.DMA((parts,)),
+            pltpu.SemaphoreType.DMA((late,)),
             pltpu.SemaphoreType.DMA((units,)),
         ]
         + [grid] * 5,
@@ -326,9 +361,83 @@
     )(*[pltpu.with_memory_space_constraint(x, pltpu.HBM) for x in arrays], pltpu.with_memory_space_constraint(gathered, pltpu.VMEM))
 
 
+def exchange_kernel(late_ref, other_ref, send_sem, recv_sem):
+    dp = lax.axis_index("dp")
+    side = {"dp": dp // CORES * CORES + 1 - dp % CORES}
+    barrier = pltpu.get_barrier_semaphore()
+    pl.semaphore_signal(barrier, inc=1, device_id=side, device_id_type=MESH)
+    pl.semaphore_wait(barrier, 1)
+    cp = pltpu.make_async_remote_copy(
+        src_ref=late_ref, dst_ref=other_ref, send_sem=send_sem, recv_sem=recv_sem, device_id=side, device_id_type=MESH
+    )
+    cp.start()
+    cp.wait()
+
+
+def exchange(arrived):
+    return pl.pallas_call(
+        exchange_kernel,
+        in_specs=[pl.BlockSpec(memory_space=pl.ANY)],
+        out_specs=pl.BlockSpec(memory_space=pl.ANY),
+        out_shape=pltpu.VMEM(arrived.shape, arrived.dtype),
+        scratch_shapes=[pltpu.SemaphoreType.DMA, pltpu.SemaphoreType.DMA],
+        compiler_params=pltpu.CompilerParams(collective_id=1, has_side_effects=True, vmem_limit_bytes=2**20),
+        cost_estimate=pl.CostEstimate(flops=1, bytes_accessed=4 * arrived.size, transcendentals=0),
+    )(pltpu.with_memory_space_constraint(arrived, pltpu.VMEM))
+
+
+def store_kernel(dp_count, tp_count, rows, _, late_ref, other_ref, engine_ref, sems):
+    planes, parts = dp_count // CORES, parts_of(rows)
+    part_rows = rows // parts
+    late = late_ref.shape[0] // part_rows
+    early = tp_count * parts - late
+    dp, t = lax.axis_index("dp"), lax.axis_index("tp")
+    z, core = dp // CORES, dp % CORES
+
+    @pl.when((z == 0) | (z == planes - 1))
+    def _():
+        plane = planes - 1 - z
+        copies = []
+        for which, (ref, owner) in enumerate([(late_ref, core), (other_ref, 1 - core)]):
+            for n in range(late):
+                unit = early + n
+                block = (plane * CORES + owner) * tp_count + mix(t, unit // parts, tp_count)
+                start = pl.multiple_of(block * rows + unit % parts * part_rows, part_rows)
+                copies.append(
+                    pltpu.make_async_copy(
+                        ref.at[pl.ds(n * part_rows, part_rows), :],
+                        engine_ref.at[pl.ds(start, part_rows), :],
+                        sems.at[which * late + n],
+                    )
+                )
+        for cp in copies:
+            cp.start()
+        for cp in copies:
+            cp.wait()
+
+
+def store(dp_count, tp_count, rows, engine, arrived, other):
+    late = late_of(tp_count, rows)
+    return pl.pallas_call(
+        functools.partial(store_kernel, dp_count, tp_count, rows),
+        in_specs=[pl.BlockSpec(memory_space=pltpu.HBM)] + [pl.BlockSpec(memory_space=pl.ANY)] * 2,
+        out_specs=pl.BlockSpec(memory_space=pltpu.HBM),
+        out_shape=jax.ShapeDtypeStruct(engine.shape, engine.dtype),
+        input_output_aliases={0: 0},
+        scratch_shapes=[pltpu.SemaphoreType.DMA((2 * late,))],
+        compiler_params=pltpu.CompilerParams(vmem_limit_bytes=2**20),
+        cost_estimate=pl.CostEstimate(flops=1, bytes_accessed=8 * arrived.size, transcendentals=0),
+    )(engine, *[pltpu.with_memory_space_constraint(x, pltpu.VMEM) for x in (arrived, other)])
+
+
 def body(dp_count, tp_count, *arrays):
-    gathered = spread(dp_count, tp_count, *arrays)
-    return tuple(local_step(arrays, gathered))
+    gathered, late = spread(dp_count, tp_count, *arrays)
+    top = dp_count - CORES
+    pairs = [(top - CORES + c, top + c) for c in range(CORES)] + [(CORES + c, c) for c in range(CORES)]
+    arrived = lax.ppermute(late, "dp", pairs)
+    new_master, new_avg, new_avg_sq, engine = local_step(arrays, gathered)
+    engine = store(dp_count, tp_count, arrays[0].shape[0], engine, arrived, exchange(arrived))
+    return new_master, new_avg, new_avg_sq, engine
 
 
 def solution(mesh):

time: 202 us -> 188 us (0.931)
  Pallas kernels: 201 us -> 184 us
  waiting for transfers between devices: 0 us -> 2.2 us
    pallas_call x1, Pallas kernels: 179 us -> 157 us  [spread(): pl.pallas_call(functools.partial(spread_kernel, dp_count, tp_count, parts...]
    pallas_call x0 -> x2, Pallas kernels: none -> 3.93 us  [the longest x1 2.58 us: exchange(): pl.pallas_call(exchange_kernel, in_specs=[pl.BlockSpec(memory_space=pl.AN...]
    ppermute x0 -> x1, waiting for transfers between devices: none -> 2.2 us  [body(): arrived = lax.ppermute(late, 'dp', pairs)]
  transfers between devices with their start and end apart: 0 -> 1, of which waited for: 0 -> 1; matrix products, arithmetic and copies ran while one was open for 0% -> 0% of each run, Pallas kernels for 0% -> 12%
where the time goes in v2:
time: 188 us
  Pallas kernels  184 us (98%)
  waiting for transfers between devices  2.2 us (1%)
    pallas_call x1, Pallas kernels, spread(): pl.pallas_call(functools.partial(spread_kernel, dp_count, tp_count, parts...  157 us
    pallas_call x1, Pallas kernels, local_step(): pl.pallas_call(step_kernel, grid=(rows // tile,), in_specs=[flat] * 4 + [...  22.4 us
  transfers between devices with their start and end apart: 1, of which 1 were waited for; matrix products, arithmetic and copies ran while one was open for 0% of the time, Pallas kernels for 12%

profile of v2, /device:TPU:0, one launch (start us, length us, event | category | flops | bytes accessed | tf_op | source)
XLA Modules:
  0.0 188.0 jit_solution(9175570631748330614)
XLA Ops:
  0.6 157.5 %shard_map.75 = (bf16[4096,2560]{1,0:T(8,128)(2,1)S(1)}, bf16[192,2560]{1,0:T(8,128)(2,1)S(1)}) custom-call(f32[128,10240]{1,0:T(8,128)} %m_ref.1, f32[128,10240]{1,0:T(8,128)} %g_ref.1, f32[128,10240]{1,0:T(8,128)} %a_ref.1, f32[128,10240]{1,0:T(8,128)} %s_ref.1), custom_call_target="tpu_custom_call" | custom-call | flops 26214400 | bytes 20971520 | tf_op jit(solution)/shard_map/pallas_call | solution.py:297
  158.1 1.3 collective-permute-start
  159.4 22.4 %shard_map.76 = (f32[128,10240]{1,0:T(8,128)}, f32[128,10240]{1,0:T(8,128)}, f32[128,10240]{1,0:T(8,128)}, bf16[4096,2560]{1,0:T(8,128)(2,1)}) custom-call(f32[128,10240]{1,0:T(8,128)} %m_ref.1, f32[128,10240]{1,0:T(8,128)} %g_ref.1, f32[128,10240]{1,0:T(8,128)} %a_ref.1, f32[128,10240]{1,0:T(8,128)} %s_ref.1, bf16[4096,2560]{1,0:T(8,128)(2,1)S(1)} %get-tuple-element.10.all_ref), custom_call_target="tpu_custom_call" | custom-call | flops 26214400 | bytes 57671680 | tf_op jit(solution)/shard_map/pallas_call | solution.py:348
  181.9 2.2 %collective-permute-done.late_ref = bf16[192,2560]{1,0:T(8,128)(2,1)S(1)} collective-permute-done((bf16[192,2560]{1,0:T(8,128)(2,1)S(1)}, bf16[192,2560]{1,0:T(8,128)(2,1)S(1)}, u32[]{:S(2)}, u32[]{:S(2)}) %collective-permute-start) | collective-permute-done | bytes 983072 | tf_op jit(solution)/shard_map/ppermute | solution.py:437
  184.1 2.6 %shard_map.77.other_ref = bf16[192,2560]{1,0:T(8,128)(2,1)S(1)} custom-call(bf16[192,2560]{1,0:T(8,128)(2,1)S(1)} %collective-permute-done.late_ref), custom_call_target="tpu_custom_call" | custom-call | flops 1 | bytes 1966080 | tf_op jit(solution)/shard_map/pallas_call | solution.py:378
  186.6 1.4 shard_map.78
Async XLA Ops:
  158.1 25.9 %collective-permute-start = (bf16[192,2560]{1,0:T(8,128)(2,1)S(1)}, bf16[192,2560]{1,0:T(8,128)(2,1)S(1)}, u32[]{:S(2)}, u32[]{:S(2)}) collective-permute-start(bf16[192,2560]{1,0:T(8,128)(2,1)S(1)} %get-tuple-element.15), channel_id=1, source_target_pairs={{16,24},{20,28},{8,0},{12,4},{17,25},{21,29},{9,1},{13,5},{18,26},... | collective-permute-start | bytes 2949128 | tf_op jit(solution)/shard_map/ppermute | solution.py:437

commit v3 on v1

--- a/solution.py
+++ b/solution.py
@@ -12,6 +12,8 @@
 HS = 128
 CORES = 2
 STEP = 16
+LAG = 2
+TAIL = (1, 1)
 MESH = pl.DeviceIdType.MESH
 
 
@@ -58,8 +60,9 @@
 
 
 def spread_kernel(dp_count, tp_count, parts, *refs):
-    sources, out_ref, held, mine, load_sem = refs[:4], refs[4], refs[5], refs[6], refs[7]
-    own_sem, flat_send, up_send, down_send, side_send, in_recv, side_recv = refs[8:]
+    count = 5 + len(late_pieces(tp_count, refs[0].shape[0]))
+    sources, (out_ref, *late_refs), (held, mine, load_sem) = refs[:4], refs[4:count], refs[count : count + 3]
+    own_sem, late_sem, given_sem, flat_send, up_send, down_send, side_send, in_recv, side_recv = refs[count + 3 :]
     planes = dp_count // CORES
     dp, t = lax.axis_index("dp"), lax.axis_index("tp")
     z, core = dp // CORES, dp % CORES
@@ -205,19 +208,86 @@
 
         going_side(here, here, z, unit).start()
 
-    @pl.loop(0, (planes - 1) * units)
+    def sides_done(plane, unit):
+        here, there = place(plane, core, unit), place(plane, 1 - core, unit)
+        going_side(here, here, plane, unit).wait_send()
+        copy(there, there, side_send.at[plane, unit], side_recv.at[plane, unit], side).wait_recv()
+
+    def settle(m):
+        distance, unit = m // units, m % units
+        below, above = z - distance, z + distance
+
+        @pl.when(below >= 0)
+        def _():
+            sides_done(below, unit)
+
+        @pl.when((above < planes) & (distance > 0))
+        def _():
+            sides_done(above, unit)
+
+    both, late, given = shares_of(tp_count, rows)
+    alone = units - late
+    total = (planes - 1) * units + both
+    first = jnp.where(core == 0, both, alone)
+    low, high = z == 1, z == planes - 2
+
+    def own_sent():
+        for h in range(parts):
+            keep(h).wait()
+        for j in range(1, tp_count):
+            for h in range(parts):
+                flat_copy(j, h).wait_send()
+
+        @pl.loop(0, units - LAG)
+        def _(unit):
+            settle(unit)
+
+        @pl.loop(0, units)
+        def _(unit):
+            here = place(z, core, unit)
+
+            @pl.when(has_up)
+            def _():
+                going_up(here, here, z, unit).wait_send()
+
+            @pl.when(has_down)
+            def _():
+                going_down(here, here, z, unit).wait_send()
+
+    def set_aside(here, which, n):
+        part = pl.ds(pl.multiple_of(n * part_rows, part_rows), part_rows)
+        return pltpu.make_async_copy(here, late_refs[which].at[part, :], late_sem.at[which, n])
+
+    def set_aside_start(here, n):
+        for which, (skip, size) in enumerate(late_pieces(tp_count, rows)):
+
+            @pl.when((n >= skip) & (n < skip + size))
+            def _():
+                set_aside(here, which, n - skip).start()
+
+    def hand_over(plane, n, target):
+        here = place(plane, 0, units - given + n)
+        return copy(here, here, given_sem.at[0, n], given_sem.at[1, n], target)
+
+    @pl.loop(units, total)
     def _(m):
-        distance, unit = m // units + 1, m % units
+        distance, unit = m // units, m % units
         below, above = z - distance, z + distance
+        keeps = (distance == planes - 2) & (unit >= first)
+        aside = keeps & (unit < first + late)
 
         @pl.when(below >= 0)
         def _():
             arrived(below, unit)
             here = place(below, core, unit)
 
-            @pl.when(has_up)
+            @pl.when(has_up & jnp.logical_not(keeps))
             def _():
                 going_up(here, here, below, unit).start()
+
+            @pl.when(has_up & aside)
+            def _():
+                set_aside_start(here, unit - first)
 
             going_side(here, here, below, unit).start()
 
@@ -226,34 +296,91 @@
             arrived(above, unit)
             here = place(above, core, unit)
 
-            @pl.when(has_down)
+            @pl.when(has_down & jnp.logical_not(keeps))
             def _():
                 going_down(here, here, above, unit).start()
 
+            @pl.when(has_down & aside)
+            def _():
+                set_aside_start(here, unit - first)
+
             going_side(here, here, above, unit).start()
 
-    for h in range(parts):
-        keep(h).wait()
-    for j in range(1, tp_count):
-        for h in range(parts):
-            flat_copy(j, h).wait_send()
-
-    @pl.loop(0, planes * units)
+        settle(m - LAG)
+
+        @pl.when(m == (planes - 1) * units)
+        def _():
+            own_sent()
+
+        given_m = m - LAG - ((planes - 1) * units - given)
+
+        @pl.when((given_m >= 0) & (given_m < given) & (core == 1))
+        def _():
+            @pl.when(high)
+            def _():
+                hand_over(0, given_m, up).start()
+
+            @pl.when(low)
+            def _():
+                hand_over(planes - 1, given_m, down).start()
+
+    @pl.loop(total - LAG, total)
+    def _(m):
+        settle(m)
+
+    @pl.when(core == 1)
+    def _():
+        for plane, ends, starts, target in ((0, z == planes - 1, high, up), (planes - 1, z == 0, low, down)):
+
+            @pl.when(ends)
+            def _():
+                @pl.loop(both, alone)
+                def _(unit):
+                    arrived(plane, unit)
+
+                for n in range(given):
+                    hand_over(plane, n, side).wait_recv()
+
+            @pl.when(starts)
+            def _():
+                for n in range(given):
+                    hand_over(plane, n, target).wait_send()
+
+    @pl.when(low | high)
+    def _():
+        for which, (_, size) in enumerate(late_pieces(tp_count, rows)):
+            for n in range(size):
+                set_aside(late_refs[which].at[pl.ds(0, part_rows), :], which, n).wait()
+
+    @pl.loop(0, jnp.where(has_up, z, 0) * units)
     def _(m):
         plane, unit = m // units, m % units
         here = place(plane, core, unit)
-        there = place(plane, 1 - core, unit)
-
-        @pl.when((plane <= z) & has_up)
+
+        @pl.when(jnp.logical_not((unit >= first) & (plane == 0) & high))
         def _():
             going_up(here, here, plane, unit).wait_send()
 
-        @pl.when((plane >= z) & has_down)
+    @pl.loop((z + 1) * units, jnp.where(has_down, planes, z + 1) * units)
+    def _(m):
+        plane, unit = m // units, m % units
+        here = place(plane, core, unit)
+
+        @pl.when(jnp.logical_not((unit >= first) & (plane == planes - 1) & low))
         def _():
             going_down(here, here, plane, unit).wait_send()
 
-        going_side(here, here, plane, unit).wait_send()
-        copy(there, there, side_send.at[plane, unit], side_recv.at[plane, unit], side).wait_recv()
+
+def shares_of(tp_count, rows):
+    units = tp_count * parts_of(rows)
+    late, given = units // 2 + 1, 1
+    return units - late - given, late, given
+
+
+def late_pieces(tp_count, rows):
+    late = shares_of(tp_count, rows)[1]
+    sizes = (late - sum(TAIL),) + TAIL
+    return [(sum(sizes[:i]), size) for i, size in enumerate(sizes)]
 
 
 def spread(dp_count, tp_count, *arrays):
@@ -263,16 +390,22 @@
     planes, units = dp_count // CORES, tp_count * parts
     grid = pltpu.SemaphoreType.DMA((planes, units))
     jobs = len(jobs_of(tp_count, rows))
+    late, pieces = shares_of(tp_count, rows)[1], late_pieces(tp_count, rows)
     return pl.pallas_call(
         functools.partial(spread_kernel, dp_count, tp_count, parts),
         in_specs=[pl.BlockSpec(memory_space=pltpu.HBM)] * 4,
-        out_specs=pl.BlockSpec(memory_space=pl.ANY),
-        out_shape=pltpu.VMEM((dp_count * tp_count * rows, width), jnp.bfloat16),
+        out_specs=[pl.BlockSpec(memory_space=pl.ANY)] * (1 + len(pieces)),
+        out_shape=[
+            pltpu.VMEM((dp_count * tp_count * rows, width), jnp.bfloat16),
+        ]
+        + [pltpu.VMEM((n * rows // parts, width), jnp.bfloat16) for _, n in pieces],
         scratch_shapes=[
             pltpu.VMEM((tp_count, 4, rows, width), jnp.float32),
             pltpu.VMEM((tp_count, rows, width), jnp.bfloat16),
             pltpu.SemaphoreType.DMA((jobs * 12,)),
             pltpu.SemaphoreType.DMA((parts,)),
+            pltpu.SemaphoreType.DMA((len(pieces), late)),
+            pltpu.SemaphoreType.DMA((2, shares_of(tp_count, rows)[2])),
             pltpu.SemaphoreType.DMA((units,)),
         ]
         + [grid] * 5,
@@ -326,9 +459,158 @@
     )(*[pltpu.with_memory_space_constraint(x, pltpu.HBM) for x in arrays], pltpu.with_memory_space_constraint(gathered, pltpu.VMEM))
 
 
+def far_unit(dp_count, tp_count, rows, ref, owner, unit):
+    planes, parts = dp_count // CORES, parts_of(rows)
+    part_rows = rows // parts
+    z, t = lax.axis_index("dp") // CORES, lax.axis_index("tp")
+    block = ((planes - 1 - z) * CORES + owner) * tp_count + mix(t, unit // parts, tp_count)
+    start = block * rows + unit % parts * part_rows
+    return ref.at[pl.ds(pl.multiple_of(start, part_rows), part_rows), :]
+
+
+def unshared_of(tp_count, rows):
+    both, late, given = shares_of(tp_count, rows)
+    units = tp_count * parts_of(rows)
+    return [(1, unit) for unit in range(both, units - late)] + [(0, unit) for unit in range(units - given, units)]
+
+
+def greet(side):
+    barrier = pltpu.get_barrier_semaphore()
+    pl.semaphore_signal(barrier, inc=1, device_id=side, device_id_type=MESH)
+    pl.semaphore_wait(barrier, 1)
+
+
+def exchange_kernel(dp_count, tp_count, rows, *refs):
+    planes, part_rows = dp_count // CORES, rows // parts_of(rows)
+    dp = lax.axis_index("dp")
+    z, core = dp // CORES, dp % CORES
+    side = {"dp": z * CORES + 1 - core}
+    greet(side)
+    late_ref, other_ref, send_sems, recv_sems = refs[0], refs[-3], refs[-2], refs[-1]
+
+    def copy(src, dst, n):
+        return pltpu.make_async_remote_copy(
+            src_ref=src,
+            dst_ref=dst,
+            send_sem=send_sems.at[n],
+            recv_sem=recv_sems.at[n],
+            device_id=side,
+            device_id_type=MESH,
+        )
+
+    both_ways = copy(late_ref, other_ref, 0)
+    missed = []
+    if len(refs) > 4:
+        all_ref, missed_ref = refs[1:3]
+        for n, (owner, unit) in enumerate(unshared_of(tp_count, rows)):
+            src = far_unit(dp_count, tp_count, rows, all_ref, owner, unit)
+            missed.append(copy(src, missed_ref.at[pl.ds(n * part_rows, part_rows), :], n + 1))
+
+    @pl.when((z == 0) | (z == planes - 1))
+    def _():
+        @pl.when(core == 1)
+        def _():
+            for cp in missed:
+                cp.start()
+
+        both_ways.start()
+
+        @pl.when(core == 1)
+        def _():
+            for cp in missed:
+                cp.wait_send()
+
+        @pl.when(core == 0)
+        def _():
+            for cp in missed:
+                cp.wait_recv()
+
+        both_ways.wait()
+
+
+def exchange(dp_count, tp_count, rows, number, arrived, *gathered):
+    shapes = [arrived.shape]
+    if gathered:
+        shapes.insert(0, (len(unshared_of(tp_count, rows)) * rows // parts_of(rows), arrived.shape[1]))
+    copies = 1 + len(unshared_of(tp_count, rows)) * len(gathered)
+    return pl.pallas_call(
+        functools.partial(exchange_kernel, dp_count, tp_count, rows),
+        in_specs=[pl.BlockSpec(memory_space=pl.ANY)] * (1 + len(gathered)),
+        out_specs=[pl.BlockSpec(memory_space=pl.ANY)] * len(shapes),
+        out_shape=[pltpu.VMEM(shape, arrived.dtype) for shape in shapes],
+        scratch_shapes=[pltpu.SemaphoreType.DMA((copies,))] * 2,
+        compiler_params=pltpu.CompilerParams(collective_id=number, has_side_effects=True, vmem_limit_bytes=2**20),
+        cost_estimate=pl.CostEstimate(flops=1, bytes_accessed=4 * arrived.size, transcendentals=0),
+    )(*[pltpu.with_memory_space_constraint(x, pltpu.VMEM) for x in (arrived, *gathered)])
+
+
+def store_kernel(dp_count, tp_count, rows, skip, _, late_ref, other_ref, *refs):
+    engine_ref, sems = refs[-2:]
+    planes, parts = dp_count // CORES, parts_of(rows)
+    part_rows = rows // parts
+    both, late, given = shares_of(tp_count, rows)
+    alone = tp_count * parts - late
+    dp = lax.axis_index("dp")
+    z, core = dp // CORES, dp % CORES
+    ends = (z == 0) | (z == planes - 1)
+
+    def put(ref, n, owner, unit, sem):
+        here = far_unit(dp_count, tp_count, rows, engine_ref, owner, unit)
+        return pltpu.make_async_copy(ref.at[pl.ds(n * part_rows, part_rows), :], here, sems.at[sem])
+
+    copies = []
+    for ref, owner in ((late_ref, core), (other_ref, 1 - core)):
+        for n in range(ref.shape[0] // part_rows):
+            copies.append(put(ref, n, owner, n + skip + both + owner * (alone - both), len(copies)))
+    missed = []
+    if len(refs) > 2:
+        missed = [put(refs[0], n, *u, len(copies) + n) for n, u in enumerate(unshared_of(tp_count, rows))]
+
+    @pl.when(ends & (core == 0))
+    def _():
+        for cp in missed:
+            cp.start()
+
+    @pl.when(ends)
+    def _():
+        for cp in copies:
+            cp.start()
+        for cp in copies:
+            cp.wait()
+
+    @pl.when(ends & (core == 0))
+    def _():
+        for cp in missed:
+            cp.wait()
+
+
+def store(dp_count, tp_count, rows, skip, engine, *late):
+    count = sum(x.shape[0] for x in late) * parts_of(rows) // rows
+    return pl.pallas_call(
+        functools.partial(store_kernel, dp_count, tp_count, rows, skip),
+        in_specs=[pl.BlockSpec(memory_space=pltpu.HBM)] + [pl.BlockSpec(memory_space=pl.ANY)] * len(late),
+        out_specs=pl.BlockSpec(memory_space=pltpu.HBM),
+        out_shape=jax.ShapeDtypeStruct(engine.shape, engine.dtype),
+        input_output_aliases={0: 0},
+        scratch_shapes=[pltpu.SemaphoreType.DMA((count,))],
+        compiler_params=pltpu.CompilerParams(vmem_limit_bytes=2**20),
+        cost_estimate=pl.CostEstimate(flops=1, bytes_accessed=8 * late[0].size, transcendentals=0),
+    )(engine, *[pltpu.with_memory_space_constraint(x, pltpu.VMEM) for x in late])
+
+
 def body(dp_count, tp_count, *arrays):
-    gathered = spread(dp_count, tp_count, *arrays)
-    return tuple(local_step(arrays, gathered))
+    rows = arrays[0].shape[0]
+    sizes = dp_count, tp_count, rows
+    gathered, *late = spread(dp_count, tp_count, *arrays)
+    top = dp_count - CORES
+    pairs = [(top - CORES + c, top + c) for c in range(CORES)] + [(CORES + c, c) for c in range(CORES)]
+    late = [lax.ppermute(x, "dp", pairs) for x in late]
+    new_master, new_avg, new_avg_sq, engine = local_step(arrays, gathered)
+    for n, (skip, _) in enumerate(late_pieces(tp_count, rows)):
+        late[n], gathered, engine = lax.optimization_barrier((late[n], gathered, engine))
+        *missed, other = exchange(*sizes, n + 1, late[n], *([gathered] if n == 0 else []))
+        engine = store(*sizes, skip, engine, late[n], other, *missed)
+    return new_master, new_avg, new_avg_sq, engine
 
 
 def solution(mesh):

time: 202 us -> 181 us (0.90)
  Pallas kernels: 201 us -> 176 us
  starting transfers between devices: 0 us -> 3.88 us
    pallas_call x1, Pallas kernels: 179 us -> 138 us  [spread(): pl.pallas_call(functools.partial(spread_kernel, dp_count, tp_count, parts...]
    pallas_call x0 -> x6, Pallas kernels: none -> 16.2 us  [the longest x3 12.8 us: exchange(): pl.pallas_call(functools.partial(exchange_kernel, dp_count, tp_count, row...]
    ppermute x0 -> x3, starting transfers between devices: none -> 3.88 us  [body(): late = [lax.ppermute(x, 'dp', pairs) for x in late]]
  transfers between devices with their start and end apart: 0 -> 3, of which waited for: 0 -> 0; matrix products, arithmetic and copies ran while one was open for 0% -> 0% of each run, Pallas kernels for 0% -> 19%
where the time goes in v3:
time: 181 us
  Pallas kernels  176 us (97%)
  starting transfers between devices  3.88 us (2%)
    pallas_call x1, Pallas kernels, spread(): pl.pallas_call(functools.partial(spread_kernel, dp_count, tp_count, parts...  138 us
    pallas_call x1, Pallas kernels, local_step(): pl.pallas_call(step_kernel, grid=(rows // tile,), in_specs=[flat] * 4 + [...  22.4 us
    pallas_call x3, Pallas kernels, exchange(): pl.pallas_call(functools.partial(exchange_kernel, dp_count, tp_count, row...  12.8 us
    ppermute x3, starting transfers between devices, body(): late = [lax.ppermute(x, 'dp', pairs) for x in late]  3.88 us
  transfers between devices with their start and end apart: 3, of which 0 were waited for; matrix products, arithmetic and copies ran while one was open for 0% of the time, Pallas kernels for 19%

profile of v3, /device:TPU:0, one launch (start us, length us, event | category | flops | bytes accessed | tf_op | source)
XLA Modules:
  0.0 181.0 jit_solution(12208734924371349647)
XLA Ops:
  0.6 137.8 %shard_map.75 = (bf16[4096,2560]{1,0:T(8,128)(2,1)S(1)}, bf16[192,2560]{1,0:T(8,128)(2,1)S(1)}, bf16[64,2560]{1,0:T(8,128)(2,1)S(1)}, bf16[64,2560]{1,0:T(8,128)(2,1)S(1)}) custom-call(f32[128,10240]{1,0:T(8,128)} %m_ref.1, f32[128,10240]{1,0:T(8,128)} %g_ref.1, f32[128,10240]{1,0:T(8,128)} %a_ref.1, f32[128,10240]{1,0:T(8,128)} %s_ref.1), custom_call_target="tpu_custom_call" | custom-call | flops 26214400 | bytes 20971520 | tf_op jit(solution)/shard_map/pallas_call | solution.py:394
  138.4 1.3 collective-permute-start.2
  139.7 1.3 collective-permute-start.1
  141.0 1.3 collective-permute-start
  142.3 22.4 %shard_map.76 = (f32[128,10240]{1,0:T(8,128)}, f32[128,10240]{1,0:T(8,128)}, f32[128,10240]{1,0:T(8,128)}, bf16[4096,2560]{1,0:T(8,128)(2,1)}) custom-call(f32[128,10240]{1,0:T(8,128)} %m_ref.1, f32[128,10240]{1,0:T(8,128)} %g_ref.1, f32[128,10240]{1,0:T(8,128)} %a_ref.1, f32[128,10240]{1,0:T(8,128)} %s_ref.1, ...), custom_call_target="tpu_custom_call" | custom-call | flops 26214400 | bytes 57671680 | tf_op jit(solution)/shard_map/pallas_call | solution.py:446
  164.8 0.0 collective-permute-done.2.refs_0_.late_ref
  164.8 7.4 %shard_map.77 = (bf16[128,2560]{1,0:T(8,128)(2,1)S(1)}, bf16[192,2560]{1,0:T(8,128)(2,1)S(1)}) custom-call(bf16[192,2560]{1,0:T(8,128)(2,1)S(1)} %collective-permute-done.2.refs_0_.late_ref, bf16[4096,2560]{1,0:T(8,128)(2,1)S(1)} %get-tuple-element.29.all_ref.refs_1_), custom_call_target="tpu_custom_call" | custom-call | flops 1 | bytes 1966080 | tf_op jit(solution)/shard_map/pallas_call | solution.py:536
  172.2 1.6 shard_map.78._
  173.8 0.0 collective-permute-done.1.refs_0_.late_ref
  173.8 2.9 %shard_map.79.other_ref = bf16[64,2560]{1,0:T(8,128)(2,1)S(1)} custom-call(bf16[64,2560]{1,0:T(8,128)(2,1)S(1)} %collective-permute-done.1.refs_0_.late_ref), custom_call_target="tpu_custom_call" | custom-call | flops 1 | bytes 655360 | tf_op jit(solution)/shard_map/pallas_call | solution.py:536
  176.7 0.9 shard_map.80._
  177.7 0.0 collective-permute-done.refs_0_.late_ref
  177.7 2.4 %shard_map.81.other_ref = bf16[64,2560]{1,0:T(8,128)(2,1)S(1)} custom-call(bf16[64,2560]{1,0:T(8,128)(2,1)S(1)} %collective-permute-done.refs_0_.late_ref), custom_call_target="tpu_custom_call" | custom-call | flops 1 | bytes 655360 | tf_op jit(solution)/shard_map/pallas_call | solution.py:536
  180.1 0.9 shard_map.82
Async XLA Ops:
  138.4 26.3 %collective-permute-start.2 = (bf16[192,2560]{1,0:T(8,128)(2,1)S(1)}, bf16[192,2560]{1,0:T(8,128)(2,1)S(1)}, u32[]{:S(2)}, u32[]{:S(2)}) collective-permute-start(bf16[192,2560]{1,0:T(8,128)(2,1)S(1)} %get-tuple-element.27), channel_id=1, source_target_pairs={{16,24},{20,28},{8,0},{12,4},{17,25},{21,29},{9,1},{13,5},{18,26},... | collective-permute-start | bytes 2949128 | tf_op jit(solution)/shard_map/ppermute | solution.py:607
  139.7 34.1 %collective-permute-start.1 = (bf16[64,2560]{1,0:T(8,128)(2,1)S(1)}, bf16[64,2560]{1,0:T(8,128)(2,1)S(1)}, u32[]{:S(2)}, u32[]{:S(2)}) collective-permute-start(bf16[64,2560]{1,0:T(8,128)(2,1)S(1)} %get-tuple-element.26), channel_id=1, source_target_pairs={{16,24},{20,28},{8,0},{12,4},{17,25},{21,29},{9,1},{13,5},{18,26},... | collective-permute-start | bytes 983048 | tf_op jit(solution)/shard_map/ppermute | solution.py:607
  141.0 36.6 %collective-permute-start = (bf16[64,2560]{1,0:T(8,128)(2,1)S(1)}, bf16[64,2560]{1,0:T(8,128)(2,1)S(1)}, u32[]{:S(2)}, u32[]{:S(2)}) collective-permute-start(bf16[64,2560]{1,0:T(8,128)(2,1)S(1)} %get-tuple-element.25), channel_id=1, source_target_pairs={{16,24},{20,28},{8,0},{12,4},{17,25},{21,29},{9,1},{13,5},{18,26},... | collective-permute-start | bytes 983048 | tf_op jit(solution)/shard_map/ppermute | solution.py:607

commit v4 on v3

--- a/solution.py
+++ b/solution.py
@@ -12,7 +12,7 @@
 HS = 128
 CORES = 2
 STEP = 16
-LAG = 2
+AHEAD = 2
 TAIL = (1, 1)
 MESH = pl.DeviceIdType.MESH
 
@@ -88,7 +88,7 @@
     def _():
         pl.semaphore_signal(barrier, inc=1, device_id=down, device_id_type=MESH)
 
-    jobs = jobs_of(tp_count, rows)
+    jobs, ahead = jobs_of(tp_count, rows), AHEAD
 
     def loads(i):
         j, first, size = jobs[i]
@@ -97,11 +97,16 @@
             pltpu.make_async_copy(
                 sources[n].at[part, pl.ds(pl.multiple_of(start, HS), width)],
                 held.at[j, n, part, pl.ds(into, width)],
-                load_sem.at[(i * 4 + n) * 3 + k],
+                load_sem.at[i % (ahead + 1)],
             )
             for n in range(4)
-            for k, (start, width, into) in enumerate(pieces_of(tp_count, mix(t, j, tp_count)))
+            for start, width, into in pieces_of(tp_count, mix(t, j, tp_count))
         ]
+
+    def loaded(i):
+        j, first, size = jobs[i]
+        all_of_it = held.at[j, :, pl.ds(first, size), :]
+        pltpu.make_async_copy(all_of_it, all_of_it, load_sem.at[i % (ahead + 1)]).wait()
 
     def compute(i):
         j, first, size = jobs[i]
@@ -131,17 +136,17 @@
         )
 
     def going_up(src, dst, plane, unit):
-        return copy(src, dst, up_send.at[plane, unit], in_recv.at[plane, unit], up)
+        return copy(src, dst, up_send.at[plane], in_recv.at[plane, unit], up)
 
     def going_down(src, dst, plane, unit):
-        return copy(src, dst, down_send.at[plane, unit], in_recv.at[plane, unit], down)
+        return copy(src, dst, down_send.at[plane], in_recv.at[plane, unit], down)
 
     def going_side(src, dst, plane, unit):
-        return copy(src, dst, side_send.at[plane, unit], side_recv.at[plane, unit], side)
+        return copy(src, dst, side_send.at[plane], side_recv.at[plane], side)
 
     def arrived(plane, unit):
         here = place(plane, core, unit)
-        copy(here, here, side_send.at[plane, unit], in_recv.at[plane, unit], side).wait_recv()
+        copy(here, here, side_send.at[plane], in_recv.at[plane, unit], side).wait_recv()
 
     def home(first, size):
         start = ((z * CORES + core) * tp_count + t) * rows + first
@@ -151,10 +156,10 @@
         part = pl.ds(h * part_rows, part_rows)
         unit = j * parts + h
         target = {"tp": mix(t, j, tp_count)}
-        return copy(mine.at[j, part, :], home(h * part_rows, part_rows), flat_send.at[unit], in_recv.at[z, unit], target)
+        return copy(mine.at[j, part, :], home(h * part_rows, part_rows), flat_send.at[0], in_recv.at[z, unit], target)
 
     def keep(h):
-        return pltpu.make_async_copy(mine.at[0, pl.ds(h * part_rows, part_rows), :], place(z, core, h), own_sem.at[h])
+        return pltpu.make_async_copy(mine.at[0, pl.ds(h * part_rows, part_rows), :], place(z, core, h), own_sem.at[0])
 
     def send(i):
         j, first, size = jobs[i]
@@ -176,13 +181,11 @@
         if (first + size) % part_rows == 0:
             keep(h).start()
 
-    ahead = 2
     for i in range(ahead):
         for cp in loads(i):
             cp.start()
     for i in range(len(jobs)):
-        for cp in loads(i):
-            cp.wait()
+        loaded(i)
         if i + ahead < len(jobs):
             for cp in loads(i + ahead):
                 cp.start()
@@ -208,55 +211,23 @@
 
         going_side(here, here, z, unit).start()
 
-    def sides_done(plane, unit):
-        here, there = place(plane, core, unit), place(plane, 1 - core, unit)
-        going_side(here, here, plane, unit).wait_send()
-        copy(there, there, side_send.at[plane, unit], side_recv.at[plane, unit], side).wait_recv()
-
-    def settle(m):
-        distance, unit = m // units, m % units
-        below, above = z - distance, z + distance
-
-        @pl.when(below >= 0)
-        def _():
-            sides_done(below, unit)
-
-        @pl.when((above < planes) & (distance > 0))
-        def _():
-            sides_done(above, unit)
-
     both, late, given = shares_of(tp_count, rows)
     alone = units - late
-    total = (planes - 1) * units + both
     first = jnp.where(core == 0, both, alone)
     low, high = z == 1, z == planes - 2
 
-    def own_sent():
-        for h in range(parts):
-            keep(h).wait()
-        for j in range(1, tp_count):
-            for h in range(parts):
-                flat_copy(j, h).wait_send()
-
-        @pl.loop(0, units - LAG)
-        def _(unit):
-            settle(unit)
-
-        @pl.loop(0, units)
-        def _(unit):
-            here = place(z, core, unit)
-
-            @pl.when(has_up)
-            def _():
-                going_up(here, here, z, unit).wait_send()
-
-            @pl.when(has_down)
-            def _():
-                going_down(here, here, z, unit).wait_send()
+    def sum_of(count, send_sem, recv_sem):
+        here = out_ref.at[pl.ds(0, count * part_rows), :]
+        return copy(here, here, send_sem, recv_sem, side)
+
+    def sides_done(plane, count):
+        done = sum_of(count, side_send.at[plane], side_recv.at[plane])
+        done.wait_send()
+        done.wait_recv()
 
     def set_aside(here, which, n):
         part = pl.ds(pl.multiple_of(n * part_rows, part_rows), part_rows)
-        return pltpu.make_async_copy(here, late_refs[which].at[part, :], late_sem.at[which, n])
+        return pltpu.make_async_copy(here, late_refs[which].at[part, :], late_sem.at[which])
 
     def set_aside_start(here, n):
         for which, (skip, size) in enumerate(late_pieces(tp_count, rows)):
@@ -269,7 +240,7 @@
         here = place(plane, 0, units - given + n)
         return copy(here, here, given_sem.at[0, n], given_sem.at[1, n], target)
 
-    @pl.loop(units, total)
+    @pl.loop(units, (planes - 1) * units)
     def _(m):
         distance, unit = m // units, m % units
         below, above = z - distance, z + distance
@@ -306,33 +277,46 @@
 
             going_side(here, here, above, unit).start()
 
-        settle(m - LAG)
-
-        @pl.when(m == (planes - 1) * units)
-        def _():
-            own_sent()
-
-        given_m = m - LAG - ((planes - 1) * units - given)
-
-        @pl.when((given_m >= 0) & (given_m < given) & (core == 1))
-        def _():
-            @pl.when(high)
-            def _():
-                hand_over(0, given_m, up).start()
-
-            @pl.when(low)
-            def _():
-                hand_over(planes - 1, given_m, down).start()
-
-    @pl.loop(total - LAG, total)
-    def _(m):
-        settle(m)
-
-    @pl.when(core == 1)
-    def _():
-        for plane, ends, starts, target in ((0, z == planes - 1, high, up), (planes - 1, z == 0, low, down)):
-
-            @pl.when(ends)
+    mine_all, flats = mine.at[0], mine.at[pl.ds(1, tp_count - 1)]
+    pltpu.make_async_copy(mine_all, mine_all, own_sem.at[0]).wait()
+    copy(flats, flats, flat_send.at[0], side_recv.at[z], side).wait_send()
+
+    @pl.when(has_up)
+    def _():
+        sum_of(units, up_send.at[z], side_recv.at[z]).wait_send()
+
+    @pl.when(has_down)
+    def _():
+        sum_of(units, down_send.at[z], side_recv.at[z]).wait_send()
+
+    far = [((z == planes - 1), 0), ((z == 0), planes - 1)]
+
+    @pl.loop(0, planes)
+    def _(plane):
+        @pl.when((plane - z < planes - 1) & (z - plane < planes - 1))
+        def _():
+            sides_done(plane, units)
+
+    for starts, plane, target in ((high, 0, up), (low, planes - 1, down)):
+
+        @pl.when(starts & (core == 1))
+        def _():
+            for n in range(given):
+                hand_over(plane, n, target).start()
+
+    for ends, plane in far:
+
+        @pl.when(ends)
+        def _():
+            @pl.loop(0, both)
+            def _(unit):
+                arrived(plane, unit)
+                here = place(plane, core, unit)
+                going_side(here, here, plane, unit).start()
+
+            sides_done(plane, both)
+
+            @pl.when(core == 1)
             def _():
                 @pl.loop(both, alone)
                 def _(unit):
@@ -341,34 +325,31 @@
                 for n in range(given):
                     hand_over(plane, n, side).wait_recv()
 
-            @pl.when(starts)
-            def _():
-                for n in range(given):
-                    hand_over(plane, n, target).wait_send()
-
-    @pl.when(low | high)
-    def _():
-        for which, (_, size) in enumerate(late_pieces(tp_count, rows)):
-            for n in range(size):
-                set_aside(late_refs[which].at[pl.ds(0, part_rows), :], which, n).wait()
-
-    @pl.loop(0, jnp.where(has_up, z, 0) * units)
-    def _(m):
-        plane, unit = m // units, m % units
-        here = place(plane, core, unit)
-
-        @pl.when(jnp.logical_not((unit >= first) & (plane == 0) & high))
-        def _():
-            going_up(here, here, plane, unit).wait_send()
-
-    @pl.loop((z + 1) * units, jnp.where(has_down, planes, z + 1) * units)
-    def _(m):
-        plane, unit = m // units, m % units
-        here = place(plane, core, unit)
-
-        @pl.when(jnp.logical_not((unit >= first) & (plane == planes - 1) & low))
-        def _():
-            going_down(here, here, plane, unit).wait_send()
+    for starts, plane, target, sems in ((high, 0, up, up_send), (low, planes - 1, down, down_send)):
+
+        @pl.when(starts)
+        def _():
+            for which, ref in enumerate(late_refs):
+                pltpu.make_async_copy(ref, ref, late_sem.at[which]).wait()
+
+            for owner, count in ((0, both), (1, alone)):
+
+                @pl.when(core == owner)
+                def _():
+                    sum_of(count, sems.at[plane], side_recv.at[plane]).wait_send()
+                    if owner == 1:
+                        for n in range(given):
+                            hand_over(plane, n, target).wait_send()
+
+    @pl.loop(0, planes)
+    def _(plane):
+        @pl.when((plane < z) & has_up & jnp.logical_not((plane == 0) & high))
+        def _():
+            sum_of(units, up_send.at[plane], side_recv.at[plane]).wait_send()
+
+        @pl.when((plane > z) & has_down & jnp.logical_not((plane == planes - 1) & low))
+        def _():
+            sum_of(units, down_send.at[plane], side_recv.at[plane]).wait_send()
 
 
 def shares_of(tp_count, rows):
@@ -388,8 +369,6 @@
     width = cols // tp_count
     parts = parts_of(rows)
     planes, units = dp_count // CORES, tp_count * parts
-    grid = pltpu.SemaphoreType.DMA((planes, units))
-    jobs = len(jobs_of(tp_count, rows))
     late, pieces = shares_of(tp_count, rows)[1], late_pieces(tp_count, rows)
     return pl.pallas_call(
         functools.partial(spread_kernel, dp_count, tp_count, parts),
@@ -402,13 +381,17 @@
         scratch_shapes=[
             pltpu.VMEM((tp_count, 4, rows, width), jnp.float32),
             pltpu.VMEM((tp_count, rows, width), jnp.bfloat16),
-            pltpu.SemaphoreType.DMA((jobs * 12,)),
-            pltpu.SemaphoreType.DMA((parts,)),
-            pltpu.SemaphoreType.DMA((len(pieces), late)),
+            pltpu.SemaphoreType.DMA((AHEAD + 1,)),
+            pltpu.SemaphoreType.DMA((1,)),
+            pltpu.SemaphoreType.DMA((len(pieces),)),
             pltpu.SemaphoreType.DMA((2, shares_of(tp_count, rows)[2])),
-            pltpu.SemaphoreType.DMA((units,)),
-        ]
-        + [grid] * 5,
+            pltpu.SemaphoreType.DMA((1,)),
+            pltpu.SemaphoreType.DMA((planes,)),
+            pltpu.SemaphoreType.DMA((planes,)),
+            pltpu.SemaphoreType.DMA((planes,)),
+            pltpu.SemaphoreType.DMA((planes, units)),
+            pltpu.SemaphoreType.DMA((planes,)),
+        ],
         compiler_params=pltpu.CompilerParams(collective_id=0, has_side_effects=True, vmem_limit_bytes=28 * 2**20),
         cost_estimate=pl.CostEstimate(flops=20 * rows * cols, bytes_accessed=16 * rows * cols, transcendentals=rows * cols),
     )(*[pltpu.with_memory_space_constraint(x, pltpu.HBM) for x in arrays])

time: 181 us -> 179 us (0.989)
  Pallas kernels: 176 us -> 174 us
    pallas_call x1, Pallas kernels: 138 us -> 136 us  [spread(): pl.pallas_call(functools.partial(spread_kernel, dp_count, tp_count, parts...]
  transfers between devices with their start and end apart: 3 -> 3, of which waited for: 0 -> 0; matrix products, arithmetic and copies ran while one was open for 0% -> 0% of each run, Pallas kernels for 19% -> 20%
where the time goes in v4:
time: 179 us
  Pallas kernels  174 us (97%)
  starting transfers between devices  3.88 us (2%)
    pallas_call x1, Pallas kernels, spread(): pl.pallas_call(functools.partial(spread_kernel, dp_count, tp_count, parts...  136 us
    pallas_call x1, Pallas kernels, local_step(): pl.pallas_call(step_kernel, grid=(rows // tile,), in_specs=[flat] * 4 + [...  22.4 us
    pallas_call x3, Pallas kernels, exchange(): pl.pallas_call(functools.partial(exchange_kernel, dp_count, tp_count, row...  12.8 us
    ppermute x3, starting transfers between devices, body(): late = [lax.ppermute(x, 'dp', pairs) for x in late]  3.88 us
  transfers between devices with their start and end apart: 3, of which 0 were waited for; matrix products, arithmetic and copies ran while one was open for 0% of the time, Pallas kernels for 20%

profile of v4, /device:TPU:0, one launch (start us, length us, event | category | flops | bytes accessed | tf_op | source)
XLA Modules:
  0.0 178.8 jit_solution(2971080782400999724)
XLA Ops:
  0.6 135.6 %shard_map.75 = (bf16[4096,2560]{1,0:T(8,128)(2,1)S(1)}, bf16[192,2560]{1,0:T(8,128)(2,1)S(1)}, bf16[64,2560]{1,0:T(8,128)(2,1)S(1)}, bf16[64,2560]{1,0:T(8,128)(2,1)S(1)}) custom-call(f32[128,10240]{1,0:T(8,128)} %m_ref.1, f32[128,10240]{1,0:T(8,128)} %g_ref.1, f32[128,10240]{1,0:T(8,128)} %a_ref.1, f32[128,10240]{1,0:T(8,128)} %s_ref.1), custom_call_target="tpu_custom_call" | custom-call | flops 26214400 | bytes 20971520 | tf_op jit(solution)/shard_map/pallas_call | solution.py:373
  136.2 1.3 collective-permute-start.2
  137.5 1.3 collective-permute-start.1
  138.8 1.3 collective-permute-start
  140.1 22.4 %shard_map.76 = (f32[128,10240]{1,0:T(8,128)}, f32[128,10240]{1,0:T(8,128)}, f32[128,10240]{1,0:T(8,128)}, bf16[4096,2560]{1,0:T(8,128)(2,1)}) custom-call(f32[128,10240]{1,0:T(8,128)} %m_ref.1, f32[128,10240]{1,0:T(8,128)} %g_ref.1, f32[128,10240]{1,0:T(8,128)} %a_ref.1, f32[128,10240]{1,0:T(8,128)} %s_ref.1, ...), custom_call_target="tpu_custom_call" | custom-call | flops 26214400 | bytes 57671680 | tf_op jit(solution)/shard_map/pallas_call | solution.py:429
  162.5 0.0 collective-permute-done.2.refs_0_.late_ref
  162.5 7.4 %shard_map.77 = (bf16[128,2560]{1,0:T(8,128)(2,1)S(1)}, bf16[192,2560]{1,0:T(8,128)(2,1)S(1)}) custom-call(bf16[192,2560]{1,0:T(8,128)(2,1)S(1)} %collective-permute-done.2.refs_0_.late_ref, bf16[4096,2560]{1,0:T(8,128)(2,1)S(1)} %get-tuple-element.29.all_ref.refs_1_), custom_call_target="tpu_custom_call" | custom-call | flops 1 | bytes 1966080 | tf_op jit(solution)/shard_map/pallas_call | solution.py:519
  170.0 1.6 shard_map.78._
  171.6 0.0 collective-permute-done.1.refs_0_.late_ref
  171.6 2.9 %shard_map.79.other_ref = bf16[64,2560]{1,0:T(8,128)(2,1)S(1)} custom-call(bf16[64,2560]{1,0:T(8,128)(2,1)S(1)} %collective-permute-done.1.refs_0_.late_ref), custom_call_target="tpu_custom_call" | custom-call | flops 1 | bytes 655360 | tf_op jit(solution)/shard_map/pallas_call | solution.py:519
  174.5 0.9 shard_map.80._
  175.4 0.0 collective-permute-done.refs_0_.late_ref
  175.4 2.5 %shard_map.81.other_ref = bf16[64,2560]{1,0:T(8,128)(2,1)S(1)} custom-call(bf16[64,2560]{1,0:T(8,128)(2,1)S(1)} %collective-permute-done.refs_0_.late_ref), custom_call_target="tpu_custom_call" | custom-call | flops 1 | bytes 655360 | tf_op jit(solution)/shard_map/pallas_call | solution.py:519
  177.9 0.9 shard_map.82
Async XLA Ops:
  136.2 26.3 %collective-permute-start.2 = (bf16[192,2560]{1,0:T(8,128)(2,1)S(1)}, bf16[192,2560]{1,0:T(8,128)(2,1)S(1)}, u32[]{:S(2)}, u32[]{:S(2)}) collective-permute-start(bf16[192,2560]{1,0:T(8,128)(2,1)S(1)} %get-tuple-element.27), channel_id=1, source_target_pairs={{16,24},{20,28},{8,0},{12,4},{17,25},{21,29},{9,1},{13,5},{18,26},... | collective-permute-start | bytes 2949128 | tf_op jit(solution)/shard_map/ppermute | solution.py:590
  137.5 34.1 %collective-permute-start.1 = (bf16[64,2560]{1,0:T(8,128)(2,1)S(1)}, bf16[64,2560]{1,0:T(8,128)(2,1)S(1)}, u32[]{:S(2)}, u32[]{:S(2)}) collective-permute-start(bf16[64,2560]{1,0:T(8,128)(2,1)S(1)} %get-tuple-element.26), channel_id=1, source_target_pairs={{16,24},{20,28},{8,0},{12,4},{17,25},{21,29},{9,1},{13,5},{18,26},... | collective-permute-start | bytes 983048 | tf_op jit(solution)/shard_map/ppermute | solution.py:590
  138.8 36.6 %collective-permute-start = (bf16[64,2560]{1,0:T(8,128)(2,1)S(1)}, bf16[64,2560]{1,0:T(8,128)(2,1)S(1)}, u32[]{:S(2)}, u32[]{:S(2)}) collective-permute-start(bf16[64,2560]{1,0:T(8,128)(2,1)S(1)} %get-tuple-element.25), channel_id=1, source_target_pairs={{16,24},{20,28},{8,0},{12,4},{17,25},{21,29},{9,1},{13,5},{18,26},... | collective-permute-start | bytes 983048 | tf_op jit(solution)/shard_map/ppermute | solution.py:590

commit v5 on v4

--- a/solution.py
+++ b/solution.py
@@ -14,6 +14,7 @@
 STEP = 16
 AHEAD = 2
 TAIL = (1, 1)
+UNSHARED = 1
 MESH = pl.DeviceIdType.MESH
 
 
@@ -76,7 +77,7 @@
     side = {"dp": z * CORES + 1 - core}
 
     barrier = pltpu.get_barrier_semaphore()
-    for j in range(1, tp_count):
+    for j in reversed(range(1, tp_count)):
         pl.semaphore_signal(barrier, inc=1, device_id={"tp": mix(t, j, tp_count)}, device_id_type=MESH)
     pl.semaphore_signal(barrier, inc=1, device_id=side, device_id_type=MESH)
 
@@ -212,7 +213,7 @@
         going_side(here, here, z, unit).start()
 
     both, late, given = shares_of(tp_count, rows)
-    alone = units - late
+    alone, shared = units - late, both - UNSHARED
     first = jnp.where(core == 0, both, alone)
     low, high = z == 1, z == planes - 2
 
@@ -308,13 +309,17 @@
 
         @pl.when(ends)
         def _():
-            @pl.loop(0, both)
+            @pl.loop(0, shared)
             def _(unit):
                 arrived(plane, unit)
                 here = place(plane, core, unit)
                 going_side(here, here, plane, unit).start()
 
-            sides_done(plane, both)
+            @pl.loop(shared, both)
+            def _(unit):
+                arrived(plane, unit)
+
+            sides_done(plane, shared)
 
             @pl.when(core == 1)
             def _():
@@ -451,10 +456,12 @@
     return ref.at[pl.ds(pl.multiple_of(start, part_rows), part_rows), :]
 
 
-def unshared_of(tp_count, rows):
+def unshared_of(tp_count, rows, core):
     both, late, given = shares_of(tp_count, rows)
     units = tp_count * parts_of(rows)
-    return [(1, unit) for unit in range(both, units - late)] + [(0, unit) for unit in range(units - given, units)]
+    if core == 0:
+        return [(0, unit) for unit in range(both - UNSHARED, both)]
+    return [(1, unit) for unit in range(both - UNSHARED, units - late)] + [(0, unit) for unit in range(units - given, units)]
 
 
 def greet(side):
@@ -482,31 +489,27 @@
         )
 
     both_ways = copy(late_ref, other_ref, 0)
-    missed = []
+    missed = ([], [])
     if len(refs) > 4:
         all_ref, missed_ref = refs[1:3]
-        for n, (owner, unit) in enumerate(unshared_of(tp_count, rows)):
-            src = far_unit(dp_count, tp_count, rows, all_ref, owner, unit)
-            missed.append(copy(src, missed_ref.at[pl.ds(n * part_rows, part_rows), :], n + 1))
+        for owner_core, copies in enumerate(missed):
+            for n, (owner, unit) in enumerate(unshared_of(tp_count, rows, owner_core)):
+                src = far_unit(dp_count, tp_count, rows, all_ref, owner, unit)
+                copies.append(copy(src, missed_ref.at[pl.ds(n * part_rows, part_rows), :], n + 1))
 
     @pl.when((z == 0) | (z == planes - 1))
     def _():
-        @pl.when(core == 1)
-        def _():
-            for cp in missed:
-                cp.start()
-
-        both_ways.start()
-
-        @pl.when(core == 1)
-        def _():
-            for cp in missed:
-                cp.wait_send()
-
-        @pl.when(core == 0)
-        def _():
-            for cp in missed:
-                cp.wait_recv()
+        for mine in range(CORES):
+
+            @pl.when(core == mine)
+            def _():
+                for cp in missed[mine]:
+                    cp.start()
+                both_ways.start()
+                for cp in missed[mine]:
+                    cp.wait_send()
+                for cp in missed[1 - mine]:
+                    cp.wait_recv()
 
         both_ways.wait()
 
@@ -514,8 +517,8 @@
 def exchange(dp_count, tp_count, rows, number, arrived, *gathered):
     shapes = [arrived.shape]
     if gathered:
-        shapes.insert(0, (len(unshared_of(tp_count, rows)) * rows // parts_of(rows), arrived.shape[1]))
-    copies = 1 + len(unshared_of(tp_count, rows)) * len(gathered)
+        shapes.insert(0, (len(unshared_of(tp_count, rows, 1)) * rows // parts_of(rows), arrived.shape[1]))
+    copies = 1 + len(unshared_of(tp_count, rows, 1)) * len(gathered)
     return pl.pallas_call(
         functools.partial(exchange_kernel, dp_count, tp_count, rows),
         in_specs=[pl.BlockSpec(memory_space=pl.ANY)] * (1 + len(gathered)),
@@ -545,26 +548,21 @@
     for ref, owner in ((late_ref, core), (other_ref, 1 - core)):
         for n in range(ref.shape[0] // part_rows):
             copies.append(put(ref, n, owner, n + skip + both + owner * (alone - both), len(copies)))
-    missed = []
+    missed = ([], [])
     if len(refs) > 2:
-        missed = [put(refs[0], n, *u, len(copies) + n) for n, u in enumerate(unshared_of(tp_count, rows))]
-
-    @pl.when(ends & (core == 0))
-    def _():
-        for cp in missed:
-            cp.start()
-
-    @pl.when(ends)
-    def _():
-        for cp in copies:
-            cp.start()
-        for cp in copies:
-            cp.wait()
-
-    @pl.when(ends & (core == 0))
-    def _():
-        for cp in missed:
-            cp.wait()
+        missed = [
+            [put(refs[0], n, *u, len(copies) + n) for n, u in enumerate(unshared_of(tp_count, rows, 1 - mine))]
+            for mine in range(CORES)
+        ]
+
+    for mine in range(CORES):
+
+        @pl.when(ends & (core == mine))
+        def _():
+            for cp in copies + missed[mine]:
+                cp.start()
+            for cp in copies + missed[mine]:
+                cp.wait()
 
 
 def store(dp_count, tp_count, rows, skip, engine, *late):

time: 179 us -> 178 us (level)
  no operation moved by 1% of the time
where the time goes in v5:
time: 178 us
  Pallas kernels  173 us (97%)
  starting transfers between devices  3.88 us (2%)
    pallas_call x1, Pallas kernels, spread(): pl.pallas_call(functools.partial(spread_kernel, dp_count, tp_count, parts...  134 us
    pallas_call x1, Pallas kernels, local_step(): pl.pallas_call(step_kernel, grid=(rows // tile,), in_specs=[flat] * 4 + [...  22.4 us
    pallas_call x3, Pallas kernels, exchange(): pl.pallas_call(functools.partial(exchange_kernel, dp_count, tp_count, row...  12.7 us
    ppermute x3, starting transfers between devices, body(): late = [lax.ppermute(x, 'dp', pairs) for x in late]  3.88 us
  transfers between devices with their start and end apart: 3, of which 0 were waited for; matrix products, arithmetic and copies ran while one was open for 0% of the time, Pallas kernels for 20%

profile of v5, /device:TPU:0, one launch (start us, length us, event | category | flops | bytes accessed | tf_op | source)
XLA Modules:
  0.0 177.5 jit_solution(6813502464634871670)
XLA Ops:
  0.6 134.3 %shard_map.75 = (bf16[4096,2560]{1,0:T(8,128)(2,1)S(1)}, bf16[192,2560]{1,0:T(8,128)(2,1)S(1)}, bf16[64,2560]{1,0:T(8,128)(2,1)S(1)}, bf16[64,2560]{1,0:T(8,128)(2,1)S(1)}) custom-call(f32[128,10240]{1,0:T(8,128)} %m_ref.1, f32[128,10240]{1,0:T(8,128)} %g_ref.1, f32[128,10240]{1,0:T(8,128)} %a_ref.1, f32[128,10240]{1,0:T(8,128)} %s_ref.1), custom_call_target="tpu_custom_call" | custom-call | flops 26214400 | bytes 20971520 | tf_op jit(solution)/shard_map/pallas_call | solution.py:378
  134.9 1.3 collective-permute-start.2
  136.2 1.3 collective-permute-start.1
  137.5 1.3 collective-permute-start
  138.8 22.4 %shard_map.76 = (f32[128,10240]{1,0:T(8,128)}, f32[128,10240]{1,0:T(8,128)}, f32[128,10240]{1,0:T(8,128)}, bf16[4096,2560]{1,0:T(8,128)(2,1)}) custom-call(f32[128,10240]{1,0:T(8,128)} %m_ref.1, f32[128,10240]{1,0:T(8,128)} %g_ref.1, f32[128,10240]{1,0:T(8,128)} %a_ref.1, f32[128,10240]{1,0:T(8,128)} %s_ref.1, ...), custom_call_target="tpu_custom_call" | custom-call | flops 26214400 | bytes 57671680 | tf_op jit(solution)/shard_map/pallas_call | solution.py:434
  161.3 0.0 collective-permute-done.2.refs_0_.late_ref
  161.3 9.2 %shard_map.77 = (bf16[192,2560]{1,0:T(8,128)(2,1)S(1)}, bf16[192,2560]{1,0:T(8,128)(2,1)S(1)}) custom-call(bf16[192,2560]{1,0:T(8,128)(2,1)S(1)} %collective-permute-done.2.refs_0_.late_ref, bf16[4096,2560]{1,0:T(8,128)(2,1)S(1)} %get-tuple-element.29.all_ref.refs_1_), custom_call_target="tpu_custom_call" | custom-call | flops 1 | bytes 1966080 | tf_op jit(solution)/shard_map/pallas_call | solution.py:522
  170.5 1.7 shard_map.78._
  172.2 0.0 collective-permute-done.1.refs_0_.late_ref
  172.2 1.7 shard_map.79.other_ref
  173.9 0.9 shard_map.80._
  174.8 0.0 collective-permute-done.refs_0_.late_ref
  174.8 1.8 %shard_map.81.other_ref = bf16[64,2560]{1,0:T(8,128)(2,1)S(1)} custom-call(bf16[64,2560]{1,0:T(8,128)(2,1)S(1)} %collective-permute-done.refs_0_.late_ref), custom_call_target="tpu_custom_call" | custom-call | flops 1 | bytes 655360 | tf_op jit(solution)/shard_map/pallas_call | solution.py:522
  176.6 0.9 shard_map.82
Async XLA Ops:
  134.9 26.3 %collective-permute-start.2 = (bf16[192,2560]{1,0:T(8,128)(2,1)S(1)}, bf16[192,2560]{1,0:T(8,128)(2,1)S(1)}, u32[]{:S(2)}, u32[]{:S(2)}) collective-permute-start(bf16[192,2560]{1,0:T(8,128)(2,1)S(1)} %get-tuple-element.27), channel_id=1, source_target_pairs={{16,24},{20,28},{8,0},{12,4},{17,25},{21,29},{9,1},{13,5},{18,26},... | collective-permute-start | bytes 2949128 | tf_op jit(solution)/shard_map/ppermute | solution.py:588
  136.2 35.9 %collective-permute-start.1 = (bf16[64,2560]{1,0:T(8,128)(2,1)S(1)}, bf16[64,2560]{1,0:T(8,128)(2,1)S(1)}, u32[]{:S(2)}, u32[]{:S(2)}) collective-permute-start(bf16[64,2560]{1,0:T(8,128)(2,1)S(1)} %get-tuple-element.26), channel_id=1, source_target_pairs={{16,24},{20,28},{8,0},{12,4},{17,25},{21,29},{9,1},{13,5},{18,26},... | collective-permute-start | bytes 983048 | tf_op jit(solution)/shard_map/ppermute | solution.py:588
  137.5 37.3 %collective-permute-start = (bf16[64,2560]{1,0:T(8,128)(2,1)S(1)}, bf16[64,2560]{1,0:T(8,128)(2,1)S(1)}, u32[]{:S(2)}, u32[]{:S(2)}) collective-permute-start(bf16[64,2560]{1,0:T(8,128)(2,1)S(1)} %get-tuple-element.25), channel_id=1, source_target_pairs={{16,24},{20,28},{8,0},{12,4},{17,25},{21,29},{9,1},{13,5},{18,26},... | collective-permute-start | bytes 983048 | tf_op jit(solution)/shard_map/ppermute | solution.py:588

commit v6 on v5

--- a/solution.py
+++ b/solution.py
@@ -12,7 +12,7 @@
 HS = 128
 CORES = 2
 STEP = 16
-AHEAD = 2
+AHEAD = 3
 TAIL = (1, 1)
 UNSHARED = 1
 MESH = pl.DeviceIdType.MESH
@@ -48,7 +48,7 @@
 def jobs_of(tp_count, rows):
     part_rows = rows // parts_of(rows)
     jobs, start = [], 0
-    first = [STEP, STEP]
+    first = [min(2 * STEP, part_rows)]
     while sum(first) < part_rows:
         first.append(min(sum(first), part_rows - sum(first)))
     for size in first + [part_rows] * (rows // part_rows - 1):
@@ -187,14 +187,14 @@
             cp.start()
     for i in range(len(jobs)):
         loaded(i)
+        compute(i)
+        if i == 1:
+            pl.semaphore_wait(barrier, tp_count + has_up.astype(jnp.int32) + has_down.astype(jnp.int32))
+        if i > 0:
+            send(i - 1)
         if i + ahead < len(jobs):
             for cp in loads(i + ahead):
                 cp.start()
-        compute(i)
-        if i == 0:
-            pl.semaphore_wait(barrier, tp_count + has_up.astype(jnp.int32) + has_down.astype(jnp.int32))
-        else:
-            send(i - 1)
     send(len(jobs) - 1)
 
     @pl.loop(parts, units)

time: 178 us -> 178 us (level)
  no operation moved by 1% of the time
where the time goes in v6:
time: 178 us; the launch traced here: 177 us
  Pallas kernels  173 us (97%)
  starting transfers between devices  3.88 us (2%)
    pallas_call x1, Pallas kernels, spread(): pl.pallas_call(functools.partial(spread_kernel, dp_count, tp_count, parts...  134 us
    pallas_call x1, Pallas kernels, local_step(): pl.pallas_call(step_kernel, grid=(rows // tile,), in_specs=[flat] * 4 + [...  22.4 us
    pallas_call x3, Pallas kernels, exchange(): pl.pallas_call(functools.partial(exchange_kernel, dp_count, tp_count, row...  12.7 us
    ppermute x3, starting transfers between devices, body(): late = [lax.ppermute(x, 'dp', pairs) for x in late]  3.88 us
  transfers between devices with their start and end apart: 3, of which 0 were waited for; matrix products, arithmetic and copies ran while one was open for 0% of the time, Pallas kernels for 20%

profile of v6, /device:TPU:0, one launch (start us, length us, event | category | flops | bytes accessed | tf_op | source)
XLA Modules:
  0.0 177.3 jit_solution(9434665392449807149)
XLA Ops:
  0.6 134.0 %shard_map.75 = (bf16[4096,2560]{1,0:T(8,128)(2,1)S(1)}, bf16[192,2560]{1,0:T(8,128)(2,1)S(1)}, bf16[64,2560]{1,0:T(8,128)(2,1)S(1)}, bf16[64,2560]{1,0:T(8,128)(2,1)S(1)}) custom-call(f32[128,10240]{1,0:T(8,128)} %m_ref.1, f32[128,10240]{1,0:T(8,128)} %g_ref.1, f32[128,10240]{1,0:T(8,128)} %a_ref.1, f32[128,10240]{1,0:T(8,128)} %s_ref.1), custom_call_target="tpu_custom_call" | custom-call | flops 26214400 | bytes 20971520 | tf_op jit(solution)/shard_map/pallas_call | solution.py:378
  134.7 1.3 collective-permute-start.2
  136.0 1.3 collective-permute-start.1
  137.3 1.3 collective-permute-start
  138.6 22.4 %shard_map.76 = (f32[128,10240]{1,0:T(8,128)}, f32[128,10240]{1,0:T(8,128)}, f32[128,10240]{1,0:T(8,128)}, bf16[4096,2560]{1,0:T(8,128)(2,1)}) custom-call(f32[128,10240]{1,0:T(8,128)} %m_ref.1, f32[128,10240]{1,0:T(8,128)} %g_ref.1, f32[128,10240]{1,0:T(8,128)} %a_ref.1, f32[128,10240]{1,0:T(8,128)} %s_ref.1, ...), custom_call_target="tpu_custom_call" | custom-call | flops 26214400 | bytes 57671680 | tf_op jit(solution)/shard_map/pallas_call | solution.py:434
  161.0 0.0 collective-permute-done.2.refs_0_.late_ref
  161.0 9.3 %shard_map.77 = (bf16[192,2560]{1,0:T(8,128)(2,1)S(1)}, bf16[192,2560]{1,0:T(8,128)(2,1)S(1)}) custom-call(bf16[192,2560]{1,0:T(8,128)(2,1)S(1)} %collective-permute-done.2.refs_0_.late_ref, bf16[4096,2560]{1,0:T(8,128)(2,1)S(1)} %get-tuple-element.29.all_ref.refs_1_), custom_call_target="tpu_custom_call" | custom-call | flops 1 | bytes 1966080 | tf_op jit(solution)/shard_map/pallas_call | solution.py:522
  170.3 1.7 shard_map.78._
  172.1 0.0 collective-permute-done.1.refs_0_.late_ref
  172.1 1.7 shard_map.79.other_ref
  173.8 0.9 shard_map.80._
  174.7 0.0 collective-permute-done.refs_0_.late_ref
  174.7 1.7 shard_map.81.other_ref
  176.4 0.9 shard_map.82
Async XLA Ops:
  134.7 26.3 %collective-permute-start.2 = (bf16[192,2560]{1,0:T(8,128)(2,1)S(1)}, bf16[192,2560]{1,0:T(8,128)(2,1)S(1)}, u32[]{:S(2)}, u32[]{:S(2)}) collective-permute-start(bf16[192,2560]{1,0:T(8,128)(2,1)S(1)} %get-tuple-element.27), channel_id=1, source_target_pairs={{16,24},{20,28},{8,0},{12,4},{17,25},{21,29},{9,1},{13,5},{18,26},... | collective-permute-start | bytes 2949128 | tf_op jit(solution)/shard_map/ppermute | solution.py:588
  136.0 36.1 %collective-permute-start.1 = (bf16[64,2560]{1,0:T(8,128)(2,1)S(1)}, bf16[64,2560]{1,0:T(8,128)(2,1)S(1)}, u32[]{:S(2)}, u32[]{:S(2)}) collective-permute-start(bf16[64,2560]{1,0:T(8,128)(2,1)S(1)} %get-tuple-element.26), channel_id=1, source_target_pairs={{16,24},{20,28},{8,0},{12,4},{17,25},{21,29},{9,1},{13,5},{18,26},... | collective-permute-start | bytes 983048 | tf_op jit(solution)/shard_map/ppermute | solution.py:588
  137.3 37.4 %collective-permute-start = (bf16[64,2560]{1,0:T(8,128)(2,1)S(1)}, bf16[64,2560]{1,0:T(8,128)(2,1)S(1)}, u32[]{:S(2)}, u32[]{:S(2)}) collective-permute-start(bf16[64,2560]{1,0:T(8,128)(2,1)S(1)} %get-tuple-element.25), channel_id=1, source_target_pairs={{16,24},{20,28},{8,0},{12,4},{17,25},{21,29},{9,1},{13,5},{18,26},... | collective-permute-start | bytes 983048 | tf_op jit(solution)/shard_map/ppermute | solution.py:588

commit v7 on v6

--- a/solution.py
+++ b/solution.py
@@ -13,8 +13,7 @@
 CORES = 2
 STEP = 16
 AHEAD = 3
-TAIL = (1, 1)
-UNSHARED = 1
+TAIL = (2, 1)
 MESH = pl.DeviceIdType.MESH
 
 
@@ -48,7 +47,7 @@
 def jobs_of(tp_count, rows):
     part_rows = rows // parts_of(rows)
     jobs, start = [], 0
-    first = [min(2 * STEP, part_rows)]
+    first = [STEP, STEP]
     while sum(first) < part_rows:
         first.append(min(sum(first), part_rows - sum(first)))
     for size in first + [part_rows] * (rows // part_rows - 1):
@@ -213,7 +212,7 @@
         going_side(here, here, z, unit).start()
 
     both, late, given = shares_of(tp_count, rows)
-    alone, shared = units - late, both - UNSHARED
+    alone = units - late
     first = jnp.where(core == 0, both, alone)
     low, high = z == 1, z == planes - 2
 
@@ -309,17 +308,9 @@
 
         @pl.when(ends)
         def _():
-            @pl.loop(0, shared)
+            @pl.loop(0, both)
             def _(unit):
                 arrived(plane, unit)
-                here = place(plane, core, unit)
-                going_side(here, here, plane, unit).start()
-
-            @pl.loop(shared, both)
-            def _(unit):
-                arrived(plane, unit)
-
-            sides_done(plane, shared)
 
             @pl.when(core == 1)
             def _():
@@ -359,7 +350,7 @@
 
 def shares_of(tp_count, rows):
     units = tp_count * parts_of(rows)
-    late, given = units // 2 + 1, 1
+    late, given = units // 2 + 2, 1
     return units - late - given, late, given
 
 
@@ -460,8 +451,8 @@
     both, late, given = shares_of(tp_count, rows)
     units = tp_count * parts_of(rows)
     if core == 0:
-        return [(0, unit) for unit in range(both - UNSHARED, both)]
-    return [(1, unit) for unit in range(both - UNSHARED, units - late)] + [(0, unit) for unit in range(units - given, units)]
+        return [(0, unit) for unit in range(both)]
+    return [(1, unit) for unit in range(units - late)] + [(0, unit) for unit in range(units - given, units)]
 
 
 def greet(side):

time: 178 us -> 178 us (level)
    pallas_call x1, Pallas kernels: 134 us -> 127 us  [spread(): pl.pallas_call(functools.partial(spread_kernel, dp_count, tp_count, parts...]
    pallas_call x3, Pallas kernels: 12.7 us -> 19.5 us  [exchange(): pl.pallas_call(functools.partial(exchange_kernel, dp_count, tp_count, row...]
  transfers between devices with their start and end apart: 3 -> 3, of which waited for: 0 -> 0; matrix products, arithmetic and copies ran while one was open for 0% -> 0% of each run, Pallas kernels for 20% -> 24%
where the time goes in v7:
time: 178 us; the launch traced here: 177 us
  Pallas kernels  173 us (97%)
  starting transfers between devices  3.88 us (2%)
    pallas_call x1, Pallas kernels, spread(): pl.pallas_call(functools.partial(spread_kernel, dp_count, tp_count, parts...  127 us
    pallas_call x1, Pallas kernels, local_step(): pl.pallas_call(step_kernel, grid=(rows // tile,), in_specs=[flat] * 4 + [...  22.4 us
    pallas_call x3, Pallas kernels, exchange(): pl.pallas_call(functools.partial(exchange_kernel, dp_count, tp_count, row...  19.5 us
    ppermute x3, starting transfers between devices, body(): late = [lax.ppermute(x, 'dp', pairs) for x in late]  3.88 us
    pallas_call x3, Pallas kernels, store(): pl.pallas_call(functools.partial(store_kernel, dp_count, tp_count, rows,...  3.74 us
  transfers between devices with their start and end apart: 3, of which 0 were waited for; matrix products, arithmetic and copies ran while one was open for 0% of the time, Pallas kernels for 24%

profile of v7, /device:TPU:0, one launch (start us, length us, event | category | flops | bytes accessed | tf_op | source)
XLA Modules:
  0.0 177.2 jit_solution(212351224732345097)
XLA Ops:
  0.6 127.0 %shard_map.75 = (bf16[4096,2560]{1,0:T(8,128)(2,1)S(1)}, bf16[192,2560]{1,0:T(8,128)(2,1)S(1)}, bf16[128,2560]{1,0:T(8,128)(2,1)S(1)}, bf16[64,2560]{1,0:T(8,128)(2,1)S(1)}) custom-call(f32[128,10240]{1,0:T(8,128)} %m_ref.1, f32[128,10240]{1,0:T(8,128)} %g_ref.1, f32[128,10240]{1,0:T(8,128)} %a_ref.1, f32[128,10240]{1,0:T(8,128)} %s_ref.1), custom_call_target="tpu_custom_call" | custom-call | flops 26214400 | bytes 20971520 | tf_op jit(solution)/shard_map/pallas_call | solution.py:369
  127.6 1.3 collective-permute-start.2
  128.9 1.3 collective-permute-start.1
  130.2 1.3 collective-permute-start
  131.5 22.4 %shard_map.76 = (f32[128,10240]{1,0:T(8,128)}, f32[128,10240]{1,0:T(8,128)}, f32[128,10240]{1,0:T(8,128)}, bf16[4096,2560]{1,0:T(8,128)(2,1)}) custom-call(f32[128,10240]{1,0:T(8,128)} %m_ref.1, f32[128,10240]{1,0:T(8,128)} %g_ref.1, f32[128,10240]{1,0:T(8,128)} %a_ref.1, f32[128,10240]{1,0:T(8,128)} %s_ref.1, ...), custom_call_target="tpu_custom_call" | custom-call | flops 26214400 | bytes 57671680 | tf_op jit(solution)/shard_map/pallas_call | solution.py:425
  154.0 0.0 collective-permute-done.2.refs_0_.late_ref
  154.0 9.3 %shard_map.77 = (bf16[192,2560]{1,0:T(8,128)(2,1)S(1)}, bf16[192,2560]{1,0:T(8,128)(2,1)S(1)}) custom-call(bf16[192,2560]{1,0:T(8,128)(2,1)S(1)} %collective-permute-done.2.refs_0_.late_ref, bf16[4096,2560]{1,0:T(8,128)(2,1)S(1)} %get-tuple-element.29.all_ref.refs_1_), custom_call_target="tpu_custom_call" | custom-call | flops 1 | bytes 1966080 | tf_op jit(solution)/shard_map/pallas_call | solution.py:513
  163.3 1.7 shard_map.78._
  165.0 0.0 collective-permute-done.1.refs_0_.late_ref
  165.0 8.2 %shard_map.79.other_ref = bf16[128,2560]{1,0:T(8,128)(2,1)S(1)} custom-call(bf16[128,2560]{1,0:T(8,128)(2,1)S(1)} %collective-permute-done.1.refs_0_.late_ref), custom_call_target="tpu_custom_call" | custom-call | flops 1 | bytes 1310720 | tf_op jit(solution)/shard_map/pallas_call | solution.py:513
  173.3 1.1 shard_map.80._
  174.4 0.0 collective-permute-done.refs_0_.late_ref
  174.4 1.9 %shard_map.81.other_ref = bf16[64,2560]{1,0:T(8,128)(2,1)S(1)} custom-call(bf16[64,2560]{1,0:T(8,128)(2,1)S(1)} %collective-permute-done.refs_0_.late_ref), custom_call_target="tpu_custom_call" | custom-call | flops 1 | bytes 655360 | tf_op jit(solution)/shard_map/pallas_call | solution.py:513
  176.3 0.9 shard_map.82
Async XLA Ops:
  127.6 26.3 %collective-permute-start.2 = (bf16[192,2560]{1,0:T(8,128)(2,1)S(1)}, bf16[192,2560]{1,0:T(8,128)(2,1)S(1)}, u32[]{:S(2)}, u32[]{:S(2)}) collective-permute-start(bf16[192,2560]{1,0:T(8,128)(2,1)S(1)} %get-tuple-element.27), channel_id=1, source_target_pairs={{16,24},{20,28},{8,0},{12,4},{17,25},{21,29},{9,1},{13,5},{18,26},... | collective-permute-start | bytes 2949128 | tf_op jit(solution)/shard_map/ppermute | solution.py:579
  128.9 36.1 %collective-permute-start.1 = (bf16[128,2560]{1,0:T(8,128)(2,1)S(1)}, bf16[128,2560]{1,0:T(8,128)(2,1)S(1)}, u32[]{:S(2)}, u32[]{:S(2)}) collective-permute-start(bf16[128,2560]{1,0:T(8,128)(2,1)S(1)} %get-tuple-element.26), channel_id=1, source_target_pairs={{16,24},{20,28},{8,0},{12,4},{17,25},{21,29},{9,1},{13,5},{18,26},... | collective-permute-start | bytes 1966088 | tf_op jit(solution)/shard_map/ppermute | solution.py:579
  130.2 44.2 %collective-permute-start = (bf16[64,2560]{1,0:T(8,128)(2,1)S(1)}, bf16[64,2560]{1,0:T(8,128)(2,1)S(1)}, u32[]{:S(2)}, u32[]{:S(2)}) collective-permute-start(bf16[64,2560]{1,0:T(8,128)(2,1)S(1)} %get-tuple-element.25), channel_id=1, source_target_pairs={{16,24},{20,28},{8,0},{12,4},{17,25},{21,29},{9,1},{13,5},{18,26},... | collective-permute-start | bytes 983048 | tf_op jit(solution)/shard_map/ppermute | solution.py:579
